TPU v7x, 32 devices: a whole 2x2x4 slice. The times are simulated.
32 devices in a mesh: row: 8 (over z, y), col: 4 (over x, core).
Axes of the slice: x: 2, y: 2, z: 4, core: 2. Of those that a mesh axis runs over, the one named last changes fastest.
Arguments:
- image_embed: float32 [4096, 1152], P(('row', 'col')), may hold values from -150 to 150, as said below
- text_embed: float32 [4096, 1152], P(('row', 'col')), may hold values from -150 to 150
- log_scale: float32 [1], replicated, may hold values from 1.8 to 2.6
- bias: float32 [1], replicated, may hold values from -6 to -3
Outputs:
- loss: float32 [1], replicated
- image_grad: float32 [4096, 1152], P(('row', 'col'))
- text_grad: float32 [4096, 1152], P(('row', 'col'))
Inputs may be any that keep to these rules, and one draw needn't show every extreme that they name: Row i of image_embed and row i of text_embed are correlated.
All inputs are finite; a program needn't handle non-finite values.
Results may differ from a plain program's by a relative error of at most 0.0046.
Values may be sent and summed in bfloat16 or wider, within the bound.
No kernel may reach another device: no remote copies, remote signals or barrier semaphores. Data moves between devices by JAX's collectives and lax.ppermute only.
A program may use at most 64 MiB of HBM per device.

v0:
```python
import functools

import jax
import jax.numpy as jnp
from jax import lax
from jax.experimental import pallas as pl
from jax.experimental.pallas import tpu as pltpu
from jax.sharding import PartitionSpec as P


GRANT = 12 << 20
LANES = 128
VMEM = pl.BlockSpec(memory_space=pltpu.VMEM)
HBM = pl.BlockSpec(memory_space=pltpu.HBM)


def moved(value, axis, target):
    count = lax.axis_size(axis)
    return lax.ppermute(value, axis, [(i, target(i)) for i in range(count)])


def kernel_call(body, outs, ins, scratch=(), in_hbm=0, out_hbm=False, flops=0):
    return pl.pallas_call(
        body,
        out_shape=outs,
        in_specs=[HBM] * in_hbm + [VMEM] * (len(ins) - in_hbm),
        out_specs=jax.tree.map(lambda _: HBM if out_hbm else VMEM, outs),
        scratch_shapes=list(scratch),
        compiler_params=pltpu.CompilerParams(vmem_limit_bytes=GRANT),
        cost_estimate=pl.CostEstimate(flops=flops, bytes_accessed=0, transcendentals=0),
    )(*ins)


def dot_t(a, b):
    return lax.dot_general(a, b, (((1,), (1,)), ((), ())), preferred_element_type=jnp.float32)


def dot_n(a, b):
    return jnp.dot(a, b, preferred_element_type=jnp.float32)


def eye_signs(rows):
    eye = lax.broadcasted_iota(jnp.int32, (rows, rows), 0) == lax.broadcasted_iota(jnp.int32, (rows, rows), 1)
    return jnp.where(eye, 1.0, -1.0).astype(jnp.float32)


def softplus(v):
    return jnp.maximum(v, 0.0) + jnp.log1p(jnp.exp(-jnp.abs(v)))


def weights(arg, sign):
    return (-sign / (1.0 + jnp.exp(-arg))).astype(jnp.bfloat16)


def logits_of(par_ref, a, b):
    return par_ref[0:1, 0:1] * dot_t(a, b) + par_ref[1:2, 0:1]


def unit_parts(values):
    inverse = 1.0 / jnp.sqrt(jnp.sum(values * values, axis=1, keepdims=True) + 1e-06)
    return values * inverse, inverse


def image_norm_kernel(raw_ref, b_ref, unit_ref, inv_ref):
    unit, inverse = unit_parts(raw_ref[...])
    b_ref[...] = unit.astype(jnp.bfloat16)
    unit_ref[...] = unit
    inv_ref[...] = jnp.broadcast_to(inverse, inv_ref.shape)


def text_parts_kernel(raw_ref, unit_ref, inv_ref):
    unit, inverse = unit_parts(raw_ref[...])
    unit_ref[...] = unit
    inv_ref[...] = jnp.broadcast_to(inverse, inv_ref.shape)


def near_kernel(count, par_ref, txt_ref, img_ref, *refs):
    texts = (txt_ref,) + refs[: count - 1]
    images = (img_ref,) + refs[count - 1 : 2 * count - 2]
    img_sum_ref, txt_sum_ref, loss_ref = refs[2 * count - 2 :]
    rows = txt_ref.shape[0]
    img_sum = txt_sum = loss = None
    for j in range(count):
        sign = eye_signs(rows) if j == 0 else -1.0
        arg = -sign * logits_of(par_ref, img_ref[...], texts[j][...])
        term = dot_n(weights(arg, sign), texts[j][...])
        img_sum = term if j == 0 else img_sum + term
        arg = -sign * logits_of(par_ref, txt_ref[...], images[j][...])
        term = dot_n(weights(arg, sign), images[j][...])
        txt_sum = term if j == 0 else txt_sum + term
        part = jnp.sum(softplus(arg), axis=0, keepdims=True)
        loss = part if j == 0 else loss + part
    img_sum_ref[...] = img_sum
    txt_sum_ref[...] = txt_sum
    loss_ref[...] = jnp.broadcast_to(jnp.sum(loss, axis=1, keepdims=True), loss_ref.shape)


def far_loss_kernel(n_img, par_ref, near_ref, *refs):
    images, texts, loss_ref = refs[:n_img], refs[n_img:-1], refs[-1]
    loss = None
    for image in images:
        for text in texts:
            part = jnp.sum(softplus(logits_of(par_ref, image[...], text[...])), axis=0, keepdims=True)
            loss = part if loss is None else loss + part
    loss_ref[...] = near_ref[...] + jnp.broadcast_to(jnp.sum(loss, axis=1, keepdims=True), loss_ref.shape)


def sum_kernel(par_ref, own_ref, carry_ref, *refs):
    total = carry_ref[...]
    for block in refs[:-1]:
        arg = logits_of(par_ref, own_ref[...], block[...])
        total = total + dot_n(weights(arg, -1.0), block[...])
    refs[-1][...] = total


def far_sum(params, own, carry, blocks):
    rows, width = own.shape
    return kernel_call(
        sum_kernel,
        jax.ShapeDtypeStruct((rows, width), jnp.float32),
        (params, own, carry, *blocks),
        flops=4 * rows * rows * width * len(blocks),
    )


def last_kernel(count, par_ref, own_ref, carry_ref, unit_ref, inv_ref, *refs):
    blocks, (out_ref, buf, sems) = refs[:count], refs[count:]
    parts = sems.shape[0]
    step = buf.shape[0] // parts
    scale = par_ref[0:1, 0:1]
    gates = [weights(logits_of(par_ref, own_ref[...], block[...]), -1.0) for block in blocks]
    copies = []
    for k in range(parts):
        at = pl.ds(k * step, step)
        total = carry_ref[at, :]
        for gate, block in zip(gates, blocks):
            total = total + dot_n(gate[k * step : (k + 1) * step, :], block[...])
        grad = scale * total
        unit = unit_ref[at, :]
        inverse = inv_ref[at, 0:1]
        buf[at, :] = inverse * (grad - jnp.sum(grad * unit, axis=1, keepdims=True) * unit)
        copy = pltpu.make_async_copy(buf.at[at], out_ref.at[at], sems.at[k])
        copy.start()
        copies.append(copy)
    for copy in copies:
        copy.wait()


def finished(params, own, carry, unit, inverse, blocks):
    rows, width = own.shape
    return kernel_call(
        functools.partial(last_kernel, len(blocks)),
        jax.ShapeDtypeStruct((rows, width), jnp.float32),
        (params, own, carry, unit, inverse, *blocks),
        [pltpu.VMEM((rows, width), jnp.float32), pltpu.SemaphoreType.DMA((4,))],
        out_hbm=True,
        flops=4 * rows * rows * width * len(blocks),
    )


def summed(value):
    hops = []
    for axis in ("col", "row", "col"):
        count = lax.axis_size(axis)
        if count & (count - 1):
            return lax.psum(value, ("row", "col"))
        steps = [1 << k for k in range(count.bit_length() - 1)]
        if axis == "col":
            steps = steps[1:] if hops else steps[:1]
        hops += [(axis, step) for step in steps]
    for axis, step in hops:
        value = value + moved(value, axis, lambda i: i ^ step)
    return value


def across(mine, cores):
    count = lax.axis_size("col")
    return [moved(mine, "col", lambda i: (i + hop * cores) % count) for hop in range(1, count // cores)]


def partners(block, cores):
    return [moved(block, "col", lambda i: i // cores * cores + (i + core) % cores) for core in range(1, cores)]


def step(image_embed, text_embed, log_scale, bias):
    rows, width = image_embed.shape
    n_row = lax.axis_size("row")
    n_col = lax.axis_size("col")
    cores = 2 if n_col % 2 == 0 else 1
    params = jnp.broadcast_to(jnp.stack([jnp.exp(log_scale), bias]), (2, LANES))
    f32 = jnp.float32
    flops = 2 * rows * rows * width

    wide = jax.ShapeDtypeStruct((rows, width), f32)
    column = jax.ShapeDtypeStruct((rows, LANES), f32)
    txt_b = unit_parts(text_embed)[0].astype(jnp.bfloat16)
    txt_far = across(txt_b, cores)
    half = jax.ShapeDtypeStruct((rows, width), jnp.bfloat16)
    img_b, img_unit, img_inv = kernel_call(image_norm_kernel, (half, wide, column), (image_embed,))
    txt_unit, txt_inv = kernel_call(text_parts_kernel, (wide, column), (text_embed,))
    img_far = across(img_b, cores)
    txt_near = partners(txt_b, cores)
    img_near = partners(img_b, cores)
    terms = jax.ShapeDtypeStruct((1, LANES), f32)
    img_sum, txt_sum, loss = kernel_call(
        functools.partial(near_kernel, cores),
        (wide, wide, terms),
        (params, txt_b, img_b, *txt_near, *img_near),
        flops=4 * flops * cores,
    )
    if txt_far:
        txt_rest = [other for block in txt_far for other in partners(block, cores)]
        loss = kernel_call(
            functools.partial(far_loss_kernel, cores),
            terms,
            (params, loss, img_b, *img_near, *txt_far),
            flops=flops * cores * len(txt_far),
        )
        img_rest = [other for block in img_far for other in partners(block, cores)]
        txt_sum = far_sum(params, txt_b, txt_sum, img_far)
    image_grad = finished(params, img_b, img_sum, img_unit, img_inv, txt_far + txt_rest)
    text_grad = finished(params, txt_b, txt_sum, txt_unit, txt_inv, img_rest)
    total = summed(loss)
    loss = total[0, :1] / (rows * n_row * n_col)
    return (loss, image_grad, text_grad)


def solution(mesh):
    in_specs = (P(("row", "col"), None), P(("row", "col"), None), P(), P())
    out_specs = (P(), P(("row", "col"), None), P(("row", "col"), None))
    return jax.shard_map(step, mesh=mesh, in_specs=in_specs, out_specs=out_specs, check_vma=False)
```

profile of v0, /device:TPU:0, one launch (start us, length us, event | category | flops | bytes accessed | tf_op | source)
XLA Modules:
  0.0 42.3 jit_solution(601330792572941388)
XLA Ops:
  0.6 1.2 %multiply_reduce_fusion = f32[128]{0:T(128)S(1)} fusion(f32[128,1152]{1,0:T(8,128)} %raw_ref.3), kind=kLoop, calls=%fused_computation.1 | loop fusion | flops 294784 | bytes 590336 | tf_op jit(solution)/shard_map/reduce_sum | solution.py:60
  1.9 0.1 multiply_convert_fusion.txt_ref.own_ref
  2.0 3.0 %collective-permute-start.2 = (bf16[128,1152]{1,0:T(8,128)(2,1)S(1)}, bf16[128,1152]{1,0:T(8,128)(2,1)S(1)}, u32[]{:S(2)}, u32[]{:S(2)}) collective-permute-start(bf16[128,1152]{1,0:T(8,128)(2,1)S(1)} %multiply_convert_fusion.txt_ref.own_ref), channel_id=1, source_target_pairs={{0,2},{1,3},{2,0},{3,1},{4,6},{5,7},{6,4},{7,5},{8,10},{9,11},{10,... | collective-permute-start | bytes 884744 | tf_op jit(solution)/shard_map/ppermute | solution.py:19
  5.1 0.2 shard_map.67
  5.2 0.9 %collective-permute-start.9 = (bf16[128,1152]{1,0:T(8,128)(2,1)S(1)}, bf16[128,1152]{1,0:T(8,128)(2,1)S(1)}, u32[]{:S(2)}, u32[]{:S(2)}) collective-permute-start(bf16[128,1152]{1,0:T(8,128)(2,1)S(1)} %get-tuple-element.11.img_ref.refs_0_.own_ref), channel_id=1, source_target_pairs={{0,2},{1,3},{2,0},{3,1},{4,6},{5,7},{6,4},{7,5},{8,10},{9,11},{10,... | collective-permute-start | bytes 884744 | tf_op jit(solution)/shard_map/ppermute | solution.py:19
  6.2 0.0 collective-permute-start
  6.2 0.5 %collective-permute-start.1 = (bf16[128,1152]{1,0:T(8,128)(2,1)S(1)}, bf16[128,1152]{1,0:T(8,128)(2,1)S(1)}, u32[]{:S(2)}, u32[]{:S(2)}) collective-permute-start(bf16[128,1152]{1,0:T(8,128)(2,1)S(1)} %get-tuple-element.11.img_ref.refs_0_.own_ref), channel_id=1, source_target_pairs={{0,1},{1,0},{2,3},{3,2},{4,5},{5,4},{6,7},{7,6},{8,9},{9,8},{10,11... | collective-permute-start | bytes 884744 | tf_op jit(solution)/shard_map/ppermute | solution.py:19
  6.7 6.2 %collective-permute-done.2.refs_2_.refs_0_ = bf16[128,1152]{1,0:T(8,128)(2,1)S(1)} collective-permute-done((bf16[128,1152]{1,0:T(8,128)(2,1)S(1)}, bf16[128,1152]{1,0:T(8,128)(2,1)S(1)}, u32[]{:S(2)}, u32[]{:S(2)}) %collective-permute-start.2) | collective-permute-done | bytes 294944 | tf_op jit(solution)/shard_map/ppermute | solution.py:19
  12.9 0.0 collective-permute-start.8
  12.9 5.5 %collective-permute-done.9.refs_0_ = bf16[128,1152]{1,0:T(8,128)(2,1)S(1)} collective-permute-done((bf16[128,1152]{1,0:T(8,128)(2,1)S(1)}, bf16[128,1152]{1,0:T(8,128)(2,1)S(1)}, u32[]{:S(2)}, u32[]{:S(2)}) %collective-permute-start.9) | collective-permute-done | bytes 294944 | tf_op jit(solution)/shard_map/ppermute | solution.py:19
  19.7 0.1 maximum_bitcast_fusion
  19.8 0.0 collective-permute-done.refs_0_
  19.8 0.0 collective-permute-done.1.refs_1_
  19.8 0.1 broadcast_in_dim.9.par_ref
  19.9 1.2 %shard_map.68 = (f32[128,1152]{1,0:T(8,128)S(1)}, f32[128,1152]{1,0:T(8,128)S(1)}, f32[1,128]{1,0:T(1,128)S(1)}) custom-call(f32[2,128]{1,0:T(2,128)S(1)} %broadcast_in_dim.9.par_ref, bf16[128,1152]{1,0:T(8,128)(2,1)S(1)} %multiply_convert_fusion.txt_ref.own_ref, bf16[128,1152]{1,0:T(8,128)(2,1)S(1)} %get-tuple-element.11.img_ref.refs_0_.own_ref, ...), custom_call_target="tpu_custom_call" | custom-call | flops 301989888 | tf_op jit(solution)/shard_map/pallas_call | solution.py:23
  21.1 0.5 %shard_map.69 = f32[1,128]{1,0:T(1,128)S(1)} custom-call(f32[2,128]{1,0:T(2,128)S(1)} %broadcast_in_dim.9.par_ref, f32[1,128]{1,0:T(1,128)S(1)} %get-tuple-element.12.near_ref, bf16[128,1152]{1,0:T(8,128)(2,1)S(1)} %get-tuple-element.11.img_ref.refs_0_.own_ref, bf16[128,1152]{1,0:T(8,128)(2,1)S(1)} %collective-permute-done.1.refs_1_, ...), custom_call_target="tpu_custom_call" | custom-call | flops 75497472 | tf_op jit(solution)/shard_map/pallas_call | solution.py:23
  21.6 0.5 %collective-permute-start.3 = (f32[1,128]{1,0:T(1,128)S(1)}, f32[1,128]{1,0:T(1,128)S(1)}, u32[]{:S(2)}, u32[]{:S(2)}) collective-permute-start(f32[1,128]{1,0:T(1,128)S(1)} %shard_map.69), channel_id=1, source_target_pairs={{0,1},{1,0},{2,3},{3,2},{4,5},{5,4},{6,7},{7,6},{8,9},{9,8},{10,11... | collective-permute-start | bytes 1544 | tf_op jit(solution)/shard_map/ppermute | solution.py:19
  22.0 0.8 %collective-permute-done.3 = f32[1,128]{1,0:T(1,128)S(1)} collective-permute-done((f32[1,128]{1,0:T(1,128)S(1)}, f32[1,128]{1,0:T(1,128)S(1)}, u32[]{:S(2)}, u32[]{:S(2)}) %collective-permute-start.3) | collective-permute-done | bytes 544 | tf_op jit(solution)/shard_map/ppermute | solution.py:19
  22.9 1.8 %collective-permute-start.4 = (f32[1,128]{1,0:T(1,128)S(1)}, f32[1,128]{1,0:T(1,128)S(1)}, u32[]{:S(2)}, u32[]{:S(2)}) collective-permute-start(f32[1,128]{1,0:T(1,128)S(1)} %add.28), channel_id=1, source_target_pairs={{0,4},{4,0},{8,12},{12,8},{16,20},{20,16},{24,28},{28,24},{1,5},{5... | collective-permute-start | bytes 1544 | tf_op jit(solution)/shard_map/ppermute | solution.py:19
  24.6 1.8 %collective-permute-done.4 = f32[1,128]{1,0:T(1,128)S(1)} collective-permute-done((f32[1,128]{1,0:T(1,128)S(1)}, f32[1,128]{1,0:T(1,128)S(1)}, u32[]{:S(2)}, u32[]{:S(2)}) %collective-permute-start.4) | collective-permute-done | bytes 544 | tf_op jit(solution)/shard_map/ppermute | solution.py:19
  26.4 1.8 %collective-permute-start.5 = (f32[1,128]{1,0:T(1,128)S(1)}, f32[1,128]{1,0:T(1,128)S(1)}, u32[]{:S(2)}, u32[]{:S(2)}) collective-permute-start(f32[1,128]{1,0:T(1,128)S(1)} %add.29), channel_id=1, source_target_pairs={{0,8},{4,12},{8,0},{12,4},{16,24},{20,28},{24,16},{28,20},{1,9},{5... | collective-permute-start | bytes 1544 | tf_op jit(solution)/shard_map/ppermute | solution.py:19
  28.3 1.7 %collective-permute-done.5 = f32[1,128]{1,0:T(1,128)S(1)} collective-permute-done((f32[1,128]{1,0:T(1,128)S(1)}, f32[1,128]{1,0:T(1,128)S(1)}, u32[]{:S(2)}, u32[]{:S(2)}) %collective-permute-start.5) | collective-permute-done | bytes 544 | tf_op jit(solution)/shard_map/ppermute | solution.py:19
  30.0 2.8 %collective-permute-start.6 = (f32[1,128]{1,0:T(1,128)S(1)}, f32[1,128]{1,0:T(1,128)S(1)}, u32[]{:S(2)}, u32[]{:S(2)}) collective-permute-start(f32[1,128]{1,0:T(1,128)S(1)} %add.30), channel_id=1, source_target_pairs={{0,16},{4,20},{8,24},{12,28},{16,0},{20,4},{24,8},{28,12},{1,17},{... | collective-permute-start | bytes 1544 | tf_op jit(solution)/shard_map/ppermute | solution.py:19
  32.9 0.1 shard_map.72
  33.0 1.5 %collective-permute-done.6 = f32[1,128]{1,0:T(1,128)S(1)} collective-permute-done((f32[1,128]{1,0:T(1,128)S(1)}, f32[1,128]{1,0:T(1,128)S(1)}, u32[]{:S(2)}, u32[]{:S(2)}) %collective-permute-start.6) | collective-permute-done | bytes 544 | tf_op jit(solution)/shard_map/ppermute | solution.py:19
  34.5 1.7 %collective-permute-start.7 = (f32[1,128]{1,0:T(1,128)S(1)}, f32[1,128]{1,0:T(1,128)S(1)}, u32[]{:S(2)}, u32[]{:S(2)}) collective-permute-start(f32[1,128]{1,0:T(1,128)S(1)} %add.31), channel_id=1, source_target_pairs={{0,2},{1,3},{2,0},{3,1},{4,6},{5,7},{6,4},{7,5},{8,10},{9,11},{10,... | collective-permute-start | bytes 1544 | tf_op jit(solution)/shard_map/ppermute | solution.py:19
  36.2 0.5 %shard_map.71.carry_ref = f32[128,1152]{1,0:T(8,128)S(1)} custom-call(f32[2,128]{1,0:T(2,128)S(1)} %broadcast_in_dim.9.par_ref, bf16[128,1152]{1,0:T(8,128)(2,1)S(1)} %multiply_convert_fusion.txt_ref.own_ref, f32[128,1152]{1,0:T(8,128)S(1)} %get-tuple-element.16.carry_ref, bf16[128,1152]{1,0:T(8,128)(2,1)S(1)} %collective-permute-done.9.refs_0_), custom_call_target="tpu_custom_call" | custom-call | flops 75497472 | tf_op jit(solution)/shard_map/pallas_call | solution.py:23
  36.8 1.3 %collective-permute-done.7 = f32[1,128]{1,0:T(1,128)S(1)} collective-permute-done((f32[1,128]{1,0:T(1,128)S(1)}, f32[1,128]{1,0:T(1,128)S(1)}, u32[]{:S(2)}, u32[]{:S(2)}) %collective-permute-start.7) | collective-permute-done | bytes 544 | tf_op jit(solution)/shard_map/ppermute | solution.py:19
  38.1 0.0 collective-permute-done.8.refs_1_
  38.1 1.6 %shard_map.70 = f32[128,1152]{1,0:T(8,128)} custom-call(f32[2,128]{1,0:T(2,128)S(1)} %broadcast_in_dim.9.par_ref, bf16[128,1152]{1,0:T(8,128)(2,1)S(1)} %get-tuple-element.11.img_ref.refs_0_.own_ref, f32[128,1152]{1,0:T(8,128)S(1)} %get-tuple-element.13.carry_ref, f32[128,1152]{1,0:T(8,128)S(1)} %get-tuple-element.14.unit_ref, ...), custom_call_target="tpu_custom_call" | custom-call | flops 150994944 | tf_op jit(solution)/shard_map/pallas_call | solution.py:23
  39.7 0.0 collective-permute-done.10.refs_0_
  39.7 1.4 %shard_map.73 = f32[128,1152]{1,0:T(8,128)} custom-call(f32[2,128]{1,0:T(2,128)S(1)} %broadcast_in_dim.9.par_ref, bf16[128,1152]{1,0:T(8,128)(2,1)S(1)} %multiply_convert_fusion.txt_ref.own_ref, f32[128,1152]{1,0:T(8,128)S(1)} %shard_map.71.carry_ref, f32[128,1152]{1,0:T(8,128)S(1)} %get-tuple-element.17.unit_ref, f32[128,128]{1,0:T(8,128)S(1)} %get-tuple-element.18.inv_ref, ...), custom_call_target="tpu_custom_call" | custom-call | flops 75497472 | tf_op jit(solution)/shard_map/pallas_call | solution.py:23
  (11 shorter events, 0.0 us)
Async XLA Ops:
  0.6 1.3 %copy-start = (f32[128,1152]{1,0:T(8,128)S(1)}, f32[128,1152]{1,0:T(8,128)}, u32[]{:S(2)}) copy-start(f32[128,1152]{1,0:T(8,128)} %raw_ref.3) | copy-start | bytes 1769476
  1.9 3.2 %copy-start.1 = (f32[128,1152]{1,0:T(8,128)S(1)}, f32[128,1152]{1,0:T(8,128)}, u32[]{:S(2)}) copy-start(f32[128,1152]{1,0:T(8,128)} %raw_ref.2) | copy-start | bytes 1769476
  2.0 10.9 %collective-permute-start.2 = (bf16[128,1152]{1,0:T(8,128)(2,1)S(1)}, bf16[128,1152]{1,0:T(8,128)(2,1)S(1)}, u32[]{:S(2)}, u32[]{:S(2)}) collective-permute-start(bf16[128,1152]{1,0:T(8,128)(2,1)S(1)} %multiply_convert_fusion.txt_ref.own_ref), channel_id=1, source_target_pairs={{0,2},{1,3},{2,0},{3,1},{4,6},{5,7},{6,4},{7,5},{8,10},{9,11},{10,... | collective-permute-start | bytes 884744 | tf_op jit(solution)/shard_map/ppermute | solution.py:19
  5.2 13.2 %collective-permute-start.9 = (bf16[128,1152]{1,0:T(8,128)(2,1)S(1)}, bf16[128,1152]{1,0:T(8,128)(2,1)S(1)}, u32[]{:S(2)}, u32[]{:S(2)}) collective-permute-start(bf16[128,1152]{1,0:T(8,128)(2,1)S(1)} %get-tuple-element.11.img_ref.refs_0_.own_ref), channel_id=1, source_target_pairs={{0,2},{1,3},{2,0},{3,1},{4,6},{5,7},{6,4},{7,5},{8,10},{9,11},{10,... | collective-permute-start | bytes 884744 | tf_op jit(solution)/shard_map/ppermute | solution.py:19
  6.2 13.6 %collective-permute-start = (bf16[128,1152]{1,0:T(8,128)(2,1)S(1)}, bf16[128,1152]{1,0:T(8,128)(2,1)S(1)}, u32[]{:S(2)}, u32[]{:S(2)}) collective-permute-start(bf16[128,1152]{1,0:T(8,128)(2,1)S(1)} %multiply_convert_fusion.txt_ref.own_ref), channel_id=1, source_target_pairs={{0,1},{1,0},{2,3},{3,2},{4,5},{5,4},{6,7},{7,6},{8,9},{9,8},{10,11... | collective-permute-start | bytes 884744 | tf_op jit(solution)/shard_map/ppermute | solution.py:19
  6.2 13.6 %collective-permute-start.1 = (bf16[128,1152]{1,0:T(8,128)(2,1)S(1)}, bf16[128,1152]{1,0:T(8,128)(2,1)S(1)}, u32[]{:S(2)}, u32[]{:S(2)}) collective-permute-start(bf16[128,1152]{1,0:T(8,128)(2,1)S(1)} %get-tuple-element.11.img_ref.refs_0_.own_ref), channel_id=1, source_target_pairs={{0,1},{1,0},{2,3},{3,2},{4,5},{5,4},{6,7},{7,6},{8,9},{9,8},{10,11... | collective-permute-start | bytes 884744 | tf_op jit(solution)/shard_map/ppermute | solution.py:19
  12.9 25.2 %collective-permute-start.8 = (bf16[128,1152]{1,0:T(8,128)(2,1)S(1)}, bf16[128,1152]{1,0:T(8,128)(2,1)S(1)}, u32[]{:S(2)}, u32[]{:S(2)}) collective-permute-start(bf16[128,1152]{1,0:T(8,128)(2,1)S(1)} %collective-permute-done.2.refs_2_.refs_0_), channel_id=1, source_target_pairs={{0,1},{1,0},{2,3},{3,2},{4,5},{5,4},{6,7},{7,6},{8,9},{9,8},{10,11... | collective-permute-start | bytes 884744 | tf_op jit(solution)/shard_map/ppermute | solution.py:19
  18.4 21.3 %collective-permute-start.10 = (bf16[128,1152]{1,0:T(8,128)(2,1)S(1)}, bf16[128,1152]{1,0:T(8,128)(2,1)S(1)}, u32[]{:S(2)}, u32[]{:S(2)}) collective-permute-start(bf16[128,1152]{1,0:T(8,128)(2,1)S(1)} %collective-permute-done.9.refs_0_), channel_id=1, source_target_pairs={{0,1},{1,0},{2,3},{3,2},{4,5},{5,4},{6,7},{7,6},{8,9},{9,8},{10,11... | collective-permute-start | bytes 884744 | tf_op jit(solution)/shard_map/ppermute | solution.py:19
  21.6 1.3 %collective-permute-start.3 = (f32[1,128]{1,0:T(1,128)S(1)}, f32[1,128]{1,0:T(1,128)S(1)}, u32[]{:S(2)}, u32[]{:S(2)}) collective-permute-start(f32[1,128]{1,0:T(1,128)S(1)} %shard_map.69), channel_id=1, source_target_pairs={{0,1},{1,0},{2,3},{3,2},{4,5},{5,4},{6,7},{7,6},{8,9},{9,8},{10,11... | collective-permute-start | bytes 1544 | tf_op jit(solution)/shard_map/ppermute | solution.py:19
  22.9 3.6 %collective-permute-start.4 = (f32[1,128]{1,0:T(1,128)S(1)}, f32[1,128]{1,0:T(1,128)S(1)}, u32[]{:S(2)}, u32[]{:S(2)}) collective-permute-start(f32[1,128]{1,0:T(1,128)S(1)} %add.28), channel_id=1, source_target_pairs={{0,4},{4,0},{8,12},{12,8},{16,20},{20,16},{24,28},{28,24},{1,5},{5... | collective-permute-start | bytes 1544 | tf_op jit(solution)/shard_map/ppermute | solution.py:19
  26.4 3.6 %collective-permute-start.5 = (f32[1,128]{1,0:T(1,128)S(1)}, f32[1,128]{1,0:T(1,128)S(1)}, u32[]{:S(2)}, u32[]{:S(2)}) collective-permute-start(f32[1,128]{1,0:T(1,128)S(1)} %add.29), channel_id=1, source_target_pairs={{0,8},{4,12},{8,0},{12,4},{16,24},{20,28},{24,16},{28,20},{1,9},{5... | collective-permute-start | bytes 1544 | tf_op jit(solution)/shard_map/ppermute | solution.py:19
  30.0 4.5 %collective-permute-start.6 = (f32[1,128]{1,0:T(1,128)S(1)}, f32[1,128]{1,0:T(1,128)S(1)}, u32[]{:S(2)}, u32[]{:S(2)}) collective-permute-start(f32[1,128]{1,0:T(1,128)S(1)} %add.30), channel_id=1, source_target_pairs={{0,16},{4,20},{8,24},{12,28},{16,0},{20,4},{24,8},{28,12},{1,17},{... | collective-permute-start | bytes 1544 | tf_op jit(solution)/shard_map/ppermute | solution.py:19
  34.5 3.6 %collective-permute-start.7 = (f32[1,128]{1,0:T(1,128)S(1)}, f32[1,128]{1,0:T(1,128)S(1)}, u32[]{:S(2)}, u32[]{:S(2)}) collective-permute-start(f32[1,128]{1,0:T(1,128)S(1)} %add.31), channel_id=1, source_target_pairs={{0,2},{1,3},{2,0},{3,1},{4,6},{5,7},{6,4},{7,5},{8,10},{9,11},{10,... | collective-permute-start | bytes 1544 | tf_op jit(solution)/shard_map/ppermute | solution.py:19
where the time goes:
time: 42.4 us; the launch traced here: 42.3 us
  waiting for transfers between devices  18.8 us (44%)
  starting transfers between devices  13.2 us (31%)
  Pallas kernels  5.52 us (13%)
  between operations  3.25 us (8%)
  other arithmetic  1.44 us (3%)
    ppermute x11, waiting for transfers between devices, moved(): return lax.ppermute(value, axis, [(i, target(i)) for i in range(count)])  18.8 us
    ppermute x11, starting transfers between devices, moved(): return lax.ppermute(value, axis, [(i, target(i)) for i in range(count)])  13.2 us
    pallas_call x7, Pallas kernels, kernel_call(): pl.pallas_call(body, out_shape=outs, in_specs=[HBM] * in_hbm + [VMEM] * (...  5.52 us
    reduce_sum x1, other arithmetic, unit_parts(): jnp.sum(values * values, axis=1, keepdims=True) + 1e-06  1.25 us
  transfers between devices with their start and end apart: 11, of which 7 were waited for; matrix products, arithmetic and copies ran while one was open for 0% of the time, Pallas kernels for 10%

commit v1 on v0

--- a/solution.py
+++ b/solution.py
@@ -15,7 +15,7 @@
 
 
 def moved(value, axis, target):
-    count = lax.axis_size(axis)
+    count = lax.psum(1, axis)
     return lax.ppermute(value, axis, [(i, target(i)) for i in range(count)])
 
 
@@ -95,14 +95,15 @@
     loss_ref[...] = jnp.broadcast_to(jnp.sum(loss, axis=1, keepdims=True), loss_ref.shape)
 
 
-def far_loss_kernel(n_img, par_ref, near_ref, *refs):
+def far_loss_kernel(n_img, pairs, par_ref, near_ref, *refs):
     images, texts, loss_ref = refs[:n_img], refs[n_img:-1], refs[-1]
     loss = None
     for image in images:
         for text in texts:
             part = jnp.sum(softplus(logits_of(par_ref, image[...], text[...])), axis=0, keepdims=True)
             loss = part if loss is None else loss + part
-    loss_ref[...] = near_ref[...] + jnp.broadcast_to(jnp.sum(loss, axis=1, keepdims=True), loss_ref.shape)
+    total = near_ref[...] + jnp.broadcast_to(jnp.sum(loss, axis=1, keepdims=True), loss_ref.shape)
+    loss_ref[...] = total / pairs
 
 
 def sum_kernel(par_ref, own_ref, carry_ref, *refs):
@@ -159,23 +160,25 @@
 
 
 def summed(value):
-    hops = []
-    for axis in ("col", "row", "col"):
-        count = lax.axis_size(axis)
-        if count & (count - 1):
-            return lax.psum(value, ("row", "col"))
-        steps = [1 << k for k in range(count.bit_length() - 1)]
-        if axis == "col":
-            steps = steps[1:] if hops else steps[:1]
-        hops += [(axis, step) for step in steps]
-    for axis, step in hops:
-        value = value + moved(value, axis, lambda i: i ^ step)
-    return value
+    n_row, n_col = lax.axis_size("row"), lax.axis_size("col")
+    if n_row & (n_row - 1) or n_col & (n_col - 1) or n_col < 2:
+        return lax.psum(value, ("row", "col"))[0, :1]
+    flips = [1]
+    flips += [n_col << k | 1 for k in range(n_row.bit_length() - 1)]
+    flips += [1 << k | 1 for k in range(1, n_col.bit_length() - 1)]
+    for flip in flips:
+        other = moved(value, ("row", "col"), lambda i: i ^ flip)
+        value = value + other
+    return value[0, :1]
 
 
 def across(mine, cores):
     count = lax.axis_size("col")
-    return [moved(mine, "col", lambda i: (i + hop * cores) % count) for hop in range(1, count // cores)]
+
+    def target(i, hop):
+        return (i // cores + hop) * cores % count + cores - 1 - i % cores
+
+    return [moved(mine, "col", lambda i: target(i, hop)) for hop in range(1, count // cores)]
 
 
 def partners(block, cores):
@@ -211,7 +214,7 @@
     if txt_far:
         txt_rest = [other for block in txt_far for other in partners(block, cores)]
         loss = kernel_call(
-            functools.partial(far_loss_kernel, cores),
+            functools.partial(far_loss_kernel, cores, rows * n_row * n_col),
             terms,
             (params, loss, img_b, *img_near, *txt_far),
             flops=flops * cores * len(txt_far),
@@ -220,9 +223,7 @@
         txt_sum = far_sum(params, txt_b, txt_sum, img_far)
     image_grad = finished(params, img_b, img_sum, img_unit, img_inv, txt_far + txt_rest)
     text_grad = finished(params, txt_b, txt_sum, txt_unit, txt_inv, img_rest)
-    total = summed(loss)
-    loss = total[0, :1] / (rows * n_row * n_col)
-    return (loss, image_grad, text_grad)
+    return (summed(loss), image_grad, text_grad)
 
 
 def solution(mesh):

time: 42.4 us -> 40.1 us (0.946)
  waiting for transfers between devices: 18.8 us -> 16.3 us
  between operations: 3.25 us -> 2.06 us
  starting transfers between devices: 13.2 us -> 14.1 us
  other arithmetic: 1.44 us -> 1.95 us
    ppermute x11, waiting for transfers between devices: 18.8 us -> 16.3 us  [moved(): return lax.ppermute(value, axis, [(i, target(i)) for i in range(count)])]
    ppermute x11, starting transfers between devices: 13.2 us -> 14.1 us  [moved(): return lax.ppermute(value, axis, [(i, target(i)) for i in range(count)])]
    add x5, other arithmetic: 0.02 us -> 0.53 us  [summed(): value = value + other]
  transfers between devices with their start and end apart: 11 -> 11, of which waited for: 7 -> 7; matrix products, arithmetic and copies ran while one was open for 0% -> 2% of each run, Pallas kernels for 10% -> 10%
where the time goes in v1:
time: 40.1 us; the launch traced here: 40 us
  waiting for transfers between devices  16.3 us (41%)
  starting transfers between devices  14.1 us (35%)
  Pallas kernels  5.5 us (14%)
  between operations  2.06 us (5%)
  other arithmetic  1.95 us (5%)
    ppermute x11, waiting for transfers between devices, moved(): return lax.ppermute(value, axis, [(i, target(i)) for i in range(count)])  16.3 us
    ppermute x11, starting transfers between devices, moved(): return lax.ppermute(value, axis, [(i, target(i)) for i in range(count)])  14.1 us
    pallas_call x7, Pallas kernels, kernel_call(): pl.pallas_call(body, out_shape=outs, in_specs=[HBM] * in_hbm + [VMEM] * (...  5.5 us
    reduce_sum x1, other arithmetic, unit_parts(): jnp.sum(values * values, axis=1, keepdims=True) + 1e-06  1.25 us
  transfers between devices with their start and end apart: 11, of which 7 were waited for; matrix products, arithmetic and copies ran while one was open for 2% of the time, Pallas kernels for 10%

profile of v1, /device:TPU:0, one launch (start us, length us, event | category | flops | bytes accessed | tf_op | source)
XLA Modules:
  0.0 40.0 jit_solution(13408093641523827095)
XLA Ops:
  0.6 1.2 %multiply_reduce_fusion = f32[128]{0:T(128)S(1)} fusion(f32[128,1152]{1,0:T(8,128)} %raw_ref.3), kind=kLoop, calls=%fused_computation.1 | loop fusion | flops 294784 | bytes 590336 | tf_op jit(solution)/shard_map/reduce_sum | solution.py:60
  1.9 0.1 multiply_convert_fusion.txt_ref.own_ref
  2.0 2.5 %collective-permute-start.2 = (bf16[128,1152]{1,0:T(8,128)(2,1)S(1)}, bf16[128,1152]{1,0:T(8,128)(2,1)S(1)}, u32[]{:S(2)}, u32[]{:S(2)}) collective-permute-start(bf16[128,1152]{1,0:T(8,128)(2,1)S(1)} %multiply_convert_fusion.txt_ref.own_ref), channel_id=1, source_target_pairs={{0,3},{1,2},{2,1},{3,0},{4,7},{5,6},{6,5},{7,4},{8,11},{9,10},{10,... | collective-permute-start | bytes 884744 | tf_op jit(solution)/shard_map/ppermute | solution.py:19
  4.5 0.2 shard_map.67
  4.7 0.9 %collective-permute-start.9 = (bf16[128,1152]{1,0:T(8,128)(2,1)S(1)}, bf16[128,1152]{1,0:T(8,128)(2,1)S(1)}, u32[]{:S(2)}, u32[]{:S(2)}) collective-permute-start(bf16[128,1152]{1,0:T(8,128)(2,1)S(1)} %get-tuple-element.11.img_ref.refs_0_.own_ref), channel_id=1, source_target_pairs={{0,3},{1,2},{2,1},{3,0},{4,7},{5,6},{6,5},{7,4},{8,11},{9,10},{10,... | collective-permute-start | bytes 884744 | tf_op jit(solution)/shard_map/ppermute | solution.py:19
  5.6 0.7 %collective-permute-start = (bf16[128,1152]{1,0:T(8,128)(2,1)S(1)}, bf16[128,1152]{1,0:T(8,128)(2,1)S(1)}, u32[]{:S(2)}, u32[]{:S(2)}) collective-permute-start(bf16[128,1152]{1,0:T(8,128)(2,1)S(1)} %multiply_convert_fusion.txt_ref.own_ref), channel_id=1, source_target_pairs={{0,1},{1,0},{2,3},{3,2},{4,5},{5,4},{6,7},{7,6},{8,9},{9,8},{10,11... | collective-permute-start | bytes 884744 | tf_op jit(solution)/shard_map/ppermute | solution.py:19
  6.3 5.6 %collective-permute-done.2.refs_2_.refs_0_ = bf16[128,1152]{1,0:T(8,128)(2,1)S(1)} collective-permute-done((bf16[128,1152]{1,0:T(8,128)(2,1)S(1)}, bf16[128,1152]{1,0:T(8,128)(2,1)S(1)}, u32[]{:S(2)}, u32[]{:S(2)}) %collective-permute-start.2) | collective-permute-done | bytes 294944 | tf_op jit(solution)/shard_map/ppermute | solution.py:19
  11.9 1.1 %collective-permute-start.8 = (bf16[128,1152]{1,0:T(8,128)(2,1)S(1)}, bf16[128,1152]{1,0:T(8,128)(2,1)S(1)}, u32[]{:S(2)}, u32[]{:S(2)}) collective-permute-start(bf16[128,1152]{1,0:T(8,128)(2,1)S(1)} %collective-permute-done.2.refs_2_.refs_0_), channel_id=1, source_target_pairs={{0,1},{1,0},{2,3},{3,2},{4,5},{5,4},{6,7},{7,6},{8,9},{9,8},{10,11... | collective-permute-start | bytes 884744 | tf_op jit(solution)/shard_map/ppermute | solution.py:19
  13.0 5.2 %collective-permute-done.9.refs_0_ = bf16[128,1152]{1,0:T(8,128)(2,1)S(1)} collective-permute-done((bf16[128,1152]{1,0:T(8,128)(2,1)S(1)}, bf16[128,1152]{1,0:T(8,128)(2,1)S(1)}, u32[]{:S(2)}, u32[]{:S(2)}) %collective-permute-start.9) | collective-permute-done | bytes 294944 | tf_op jit(solution)/shard_map/ppermute | solution.py:19
  18.2 0.1 collective-permute-start.10
  19.6 0.1 maximum_bitcast_fusion
  19.7 0.0 collective-permute-done.refs_0_
  19.7 0.0 collective-permute-done.1.refs_1_
  19.7 0.1 broadcast_in_dim.9.par_ref
  19.8 1.2 %shard_map.68 = (f32[128,1152]{1,0:T(8,128)S(1)}, f32[128,1152]{1,0:T(8,128)S(1)}, f32[1,128]{1,0:T(1,128)S(1)}) custom-call(f32[2,128]{1,0:T(2,128)S(1)} %broadcast_in_dim.9.par_ref, bf16[128,1152]{1,0:T(8,128)(2,1)S(1)} %multiply_convert_fusion.txt_ref.own_ref, bf16[128,1152]{1,0:T(8,128)(2,1)S(1)} %get-tuple-element.11.img_ref.refs_0_.own_ref, ...), custom_call_target="tpu_custom_call" | custom-call | flops 301989888 | tf_op jit(solution)/shard_map/pallas_call | solution.py:23
  21.0 0.5 %shard_map.69 = f32[1,128]{1,0:T(1,128)S(1)} custom-call(f32[2,128]{1,0:T(2,128)S(1)} %broadcast_in_dim.9.par_ref, f32[1,128]{1,0:T(1,128)S(1)} %get-tuple-element.12.near_ref, bf16[128,1152]{1,0:T(8,128)(2,1)S(1)} %get-tuple-element.11.img_ref.refs_0_.own_ref, bf16[128,1152]{1,0:T(8,128)(2,1)S(1)} %collective-permute-done.1.refs_1_, ...), custom_call_target="tpu_custom_call" | custom-call | flops 75497472 | tf_op jit(solution)/shard_map/pallas_call | solution.py:23
  21.5 0.4 %collective-permute-start.3 = (f32[1,128]{1,0:T(1,128)S(1)}, f32[1,128]{1,0:T(1,128)S(1)}, u32[]{:S(2)}, u32[]{:S(2)}) collective-permute-start(f32[1,128]{1,0:T(1,128)S(1)} %shard_map.69), channel_id=1, source_target_pairs={{0,1},{1,0},{2,3},{3,2},{4,5},{5,4},{6,7},{7,6},{8,9},{9,8},{10,11... | collective-permute-start | bytes 1544 | tf_op jit(solution)/shard_map/ppermute | solution.py:19
  21.9 0.8 %collective-permute-done.3 = f32[1,128]{1,0:T(1,128)S(1)} collective-permute-done((f32[1,128]{1,0:T(1,128)S(1)}, f32[1,128]{1,0:T(1,128)S(1)}, u32[]{:S(2)}, u32[]{:S(2)}) %collective-permute-start.3) | collective-permute-done | bytes 544 | tf_op jit(solution)/shard_map/ppermute | solution.py:19
  22.7 2.4 %collective-permute-start.4 = (f32[1,128]{1,0:T(1,128)S(1)}, f32[1,128]{1,0:T(1,128)S(1)}, u32[]{:S(2)}, u32[]{:S(2)}) collective-permute-start(f32[1,128]{1,0:T(1,128)S(1)} %add.28), channel_id=1, source_target_pairs={{0,5},{1,4},{2,7},{3,6},{4,1},{5,0},{6,3},{7,2},{8,13},{9,12},{10,... | collective-permute-start | bytes 1544 | tf_op jit(solution)/shard_map/ppermute | solution.py:19
  25.1 1.3 %collective-permute-done.4 = f32[1,128]{1,0:T(1,128)S(1)} collective-permute-done((f32[1,128]{1,0:T(1,128)S(1)}, f32[1,128]{1,0:T(1,128)S(1)}, u32[]{:S(2)}, u32[]{:S(2)}) %collective-permute-start.4) | collective-permute-done | bytes 544 | tf_op jit(solution)/shard_map/ppermute | solution.py:19
  26.4 1.7 %collective-permute-start.5 = (f32[1,128]{1,0:T(1,128)S(1)}, f32[1,128]{1,0:T(1,128)S(1)}, u32[]{:S(2)}, u32[]{:S(2)}) collective-permute-start(f32[1,128]{1,0:T(1,128)S(1)} %add.29), channel_id=1, source_target_pairs={{0,9},{1,8},{2,11},{3,10},{4,13},{5,12},{6,15},{7,14},{8,1},{9,0},... | collective-permute-start | bytes 1544 | tf_op jit(solution)/shard_map/ppermute | solution.py:19
  28.2 1.3 %collective-permute-done.5 = f32[1,128]{1,0:T(1,128)S(1)} collective-permute-done((f32[1,128]{1,0:T(1,128)S(1)}, f32[1,128]{1,0:T(1,128)S(1)}, u32[]{:S(2)}, u32[]{:S(2)}) %collective-permute-start.5) | collective-permute-done | bytes 544 | tf_op jit(solution)/shard_map/ppermute | solution.py:19
  29.5 2.7 %collective-permute-start.6 = (f32[1,128]{1,0:T(1,128)S(1)}, f32[1,128]{1,0:T(1,128)S(1)}, u32[]{:S(2)}, u32[]{:S(2)}) collective-permute-start(f32[1,128]{1,0:T(1,128)S(1)} %add.30), channel_id=1, source_target_pairs={{0,17},{1,16},{2,19},{3,18},{4,21},{5,20},{6,23},{7,22},{8,25},{9,... | collective-permute-start | bytes 1544 | tf_op jit(solution)/shard_map/ppermute | solution.py:19
  32.2 0.1 shard_map.72
  32.3 1.1 %collective-permute-done.6 = f32[1,128]{1,0:T(1,128)S(1)} collective-permute-done((f32[1,128]{1,0:T(1,128)S(1)}, f32[1,128]{1,0:T(1,128)S(1)}, u32[]{:S(2)}, u32[]{:S(2)}) %collective-permute-start.6) | collective-permute-done | bytes 544 | tf_op jit(solution)/shard_map/ppermute | solution.py:19
  33.5 1.5 %collective-permute-start.7 = (f32[1,128]{1,0:T(1,128)S(1)}, f32[1,128]{1,0:T(1,128)S(1)}, u32[]{:S(2)}, u32[]{:S(2)}) collective-permute-start(f32[1,128]{1,0:T(1,128)S(1)} %add.31), channel_id=1, source_target_pairs={{0,3},{1,2},{2,1},{3,0},{4,7},{5,6},{6,5},{7,4},{8,11},{9,10},{10,... | collective-permute-start | bytes 1544 | tf_op jit(solution)/shard_map/ppermute | solution.py:19
  35.0 0.5 %shard_map.71.carry_ref = f32[128,1152]{1,0:T(8,128)S(1)} custom-call(f32[2,128]{1,0:T(2,128)S(1)} %broadcast_in_dim.9.par_ref, bf16[128,1152]{1,0:T(8,128)(2,1)S(1)} %multiply_convert_fusion.txt_ref.own_ref, f32[128,1152]{1,0:T(8,128)S(1)} %get-tuple-element.16.carry_ref, bf16[128,1152]{1,0:T(8,128)(2,1)S(1)} %collective-permute-done.9.refs_0_), custom_call_target="tpu_custom_call" | custom-call | flops 75497472 | tf_op jit(solution)/shard_map/pallas_call | solution.py:23
  35.6 0.9 %collective-permute-done.7 = f32[1,128]{1,0:T(1,128)S(1)} collective-permute-done((f32[1,128]{1,0:T(1,128)S(1)}, f32[1,128]{1,0:T(1,128)S(1)}, u32[]{:S(2)}, u32[]{:S(2)}) %collective-permute-start.7) | collective-permute-done | bytes 544 | tf_op jit(solution)/shard_map/ppermute | solution.py:19
  36.5 0.5 %add.32 = f32[1,128]{1,0:T(1,128)} add(f32[1,128]{1,0:T(1,128)S(1)} %add.31, f32[1,128]{1,0:T(1,128)S(1)} %collective-permute-done.7) | non-fusion elementwise | flops 128 | bytes 1536 | tf_op jit(solution)/shard_map/add | solution.py:171
  37.0 0.0 collective-permute-done.8.refs_1_
  37.0 1.6 %shard_map.70 = f32[128,1152]{1,0:T(8,128)} custom-call(f32[2,128]{1,0:T(2,128)S(1)} %broadcast_in_dim.9.par_ref, bf16[128,1152]{1,0:T(8,128)(2,1)S(1)} %get-tuple-element.11.img_ref.refs_0_.own_ref, f32[128,1152]{1,0:T(8,128)S(1)} %get-tuple-element.13.carry_ref, f32[128,1152]{1,0:T(8,128)S(1)} %get-tuple-element.14.unit_ref, ...), custom_call_target="tpu_custom_call" | custom-call | flops 150994944 | tf_op jit(solution)/shard_map/pallas_call | solution.py:23
  38.5 1.4 %shard_map.73 = f32[128,1152]{1,0:T(8,128)} custom-call(f32[2,128]{1,0:T(2,128)S(1)} %broadcast_in_dim.9.par_ref, bf16[128,1152]{1,0:T(8,128)(2,1)S(1)} %multiply_convert_fusion.txt_ref.own_ref, f32[128,1152]{1,0:T(8,128)S(1)} %shard_map.71.carry_ref, f32[128,1152]{1,0:T(8,128)S(1)} %get-tuple-element.17.unit_ref, f32[128,128]{1,0:T(8,128)S(1)} %get-tuple-element.18.inv_ref, ...), custom_call_target="tpu_custom_call" | custom-call | flops 75497472 | tf_op jit(solution)/shard_map/pallas_call | solution.py:23
  (11 shorter events, 0.0 us)
Async XLA Ops:
  0.6 1.3 %copy-start = (f32[128,1152]{1,0:T(8,128)S(1)}, f32[128,1152]{1,0:T(8,128)}, u32[]{:S(2)}) copy-start(f32[128,1152]{1,0:T(8,128)} %raw_ref.3) | copy-start | bytes 1769476
  1.9 2.6 %copy-start.1 = (f32[128,1152]{1,0:T(8,128)S(1)}, f32[128,1152]{1,0:T(8,128)}, u32[]{:S(2)}) copy-start(f32[128,1152]{1,0:T(8,128)} %raw_ref.2) | copy-start | bytes 1769476
  2.0 9.9 %collective-permute-start.2 = (bf16[128,1152]{1,0:T(8,128)(2,1)S(1)}, bf16[128,1152]{1,0:T(8,128)(2,1)S(1)}, u32[]{:S(2)}, u32[]{:S(2)}) collective-permute-start(bf16[128,1152]{1,0:T(8,128)(2,1)S(1)} %multiply_convert_fusion.txt_ref.own_ref), channel_id=1, source_target_pairs={{0,3},{1,2},{2,1},{3,0},{4,7},{5,6},{6,5},{7,4},{8,11},{9,10},{10,... | collective-permute-start | bytes 884744 | tf_op jit(solution)/shard_map/ppermute | solution.py:19
  4.7 13.5 %collective-permute-start.9 = (bf16[128,1152]{1,0:T(8,128)(2,1)S(1)}, bf16[128,1152]{1,0:T(8,128)(2,1)S(1)}, u32[]{:S(2)}, u32[]{:S(2)}) collective-permute-start(bf16[128,1152]{1,0:T(8,128)(2,1)S(1)} %get-tuple-element.11.img_ref.refs_0_.own_ref), channel_id=1, source_target_pairs={{0,3},{1,2},{2,1},{3,0},{4,7},{5,6},{6,5},{7,4},{8,11},{9,10},{10,... | collective-permute-start | bytes 884744 | tf_op jit(solution)/shard_map/ppermute | solution.py:19
  5.6 14.1 %collective-permute-start = (bf16[128,1152]{1,0:T(8,128)(2,1)S(1)}, bf16[128,1152]{1,0:T(8,128)(2,1)S(1)}, u32[]{:S(2)}, u32[]{:S(2)}) collective-permute-start(bf16[128,1152]{1,0:T(8,128)(2,1)S(1)} %multiply_convert_fusion.txt_ref.own_ref), channel_id=1, source_target_pairs={{0,1},{1,0},{2,3},{3,2},{4,5},{5,4},{6,7},{7,6},{8,9},{9,8},{10,11... | collective-permute-start | bytes 884744 | tf_op jit(solution)/shard_map/ppermute | solution.py:19
  6.3 13.4 %collective-permute-start.1 = (bf16[128,1152]{1,0:T(8,128)(2,1)S(1)}, bf16[128,1152]{1,0:T(8,128)(2,1)S(1)}, u32[]{:S(2)}, u32[]{:S(2)}) collective-permute-start(bf16[128,1152]{1,0:T(8,128)(2,1)S(1)} %get-tuple-element.11.img_ref.refs_0_.own_ref), channel_id=1, source_target_pairs={{0,1},{1,0},{2,3},{3,2},{4,5},{5,4},{6,7},{7,6},{8,9},{9,8},{10,11... | collective-permute-start | bytes 884744 | tf_op jit(solution)/shard_map/ppermute | solution.py:19
  11.9 25.1 %collective-permute-start.8 = (bf16[128,1152]{1,0:T(8,128)(2,1)S(1)}, bf16[128,1152]{1,0:T(8,128)(2,1)S(1)}, u32[]{:S(2)}, u32[]{:S(2)}) collective-permute-start(bf16[128,1152]{1,0:T(8,128)(2,1)S(1)} %collective-permute-done.2.refs_2_.refs_0_), channel_id=1, source_target_pairs={{0,1},{1,0},{2,3},{3,2},{4,5},{5,4},{6,7},{7,6},{8,9},{9,8},{10,11... | collective-permute-start | bytes 884744 | tf_op jit(solution)/shard_map/ppermute | solution.py:19
  18.2 20.3 %collective-permute-start.10 = (bf16[128,1152]{1,0:T(8,128)(2,1)S(1)}, bf16[128,1152]{1,0:T(8,128)(2,1)S(1)}, u32[]{:S(2)}, u32[]{:S(2)}) collective-permute-start(bf16[128,1152]{1,0:T(8,128)(2,1)S(1)} %collective-permute-done.9.refs_0_), channel_id=1, source_target_pairs={{0,1},{1,0},{2,3},{3,2},{4,5},{5,4},{6,7},{7,6},{8,9},{9,8},{10,11... | collective-permute-start | bytes 884744 | tf_op jit(solution)/shard_map/ppermute | solution.py:19
  21.5 1.2 %collective-permute-start.3 = (f32[1,128]{1,0:T(1,128)S(1)}, f32[1,128]{1,0:T(1,128)S(1)}, u32[]{:S(2)}, u32[]{:S(2)}) collective-permute-start(f32[1,128]{1,0:T(1,128)S(1)} %shard_map.69), channel_id=1, source_target_pairs={{0,1},{1,0},{2,3},{3,2},{4,5},{5,4},{6,7},{7,6},{8,9},{9,8},{10,11... | collective-permute-start | bytes 1544 | tf_op jit(solution)/shard_map/ppermute | solution.py:19
  22.7 3.7 %collective-permute-start.4 = (f32[1,128]{1,0:T(1,128)S(1)}, f32[1,128]{1,0:T(1,128)S(1)}, u32[]{:S(2)}, u32[]{:S(2)}) collective-permute-start(f32[1,128]{1,0:T(1,128)S(1)} %add.28), channel_id=1, source_target_pairs={{0,5},{1,4},{2,7},{3,6},{4,1},{5,0},{6,3},{7,2},{8,13},{9,12},{10,... | collective-permute-start | bytes 1544 | tf_op jit(solution)/shard_map/ppermute | solution.py:19
  26.4 3.0 %collective-permute-start.5 = (f32[1,128]{1,0:T(1,128)S(1)}, f32[1,128]{1,0:T(1,128)S(1)}, u32[]{:S(2)}, u32[]{:S(2)}) collective-permute-start(f32[1,128]{1,0:T(1,128)S(1)} %add.29), channel_id=1, source_target_pairs={{0,9},{1,8},{2,11},{3,10},{4,13},{5,12},{6,15},{7,14},{8,1},{9,0},... | collective-permute-start | bytes 1544 | tf_op jit(solution)/shard_map/ppermute | solution.py:19
  29.5 4.0 %collective-permute-start.6 = (f32[1,128]{1,0:T(1,128)S(1)}, f32[1,128]{1,0:T(1,128)S(1)}, u32[]{:S(2)}, u32[]{:S(2)}) collective-permute-start(f32[1,128]{1,0:T(1,128)S(1)} %add.30), channel_id=1, source_target_pairs={{0,17},{1,16},{2,19},{3,18},{4,21},{5,20},{6,23},{7,22},{8,25},{9,... | collective-permute-start | bytes 1544 | tf_op jit(solution)/shard_map/ppermute | solution.py:19
  33.5 3.0 %collective-permute-start.7 = (f32[1,128]{1,0:T(1,128)S(1)}, f32[1,128]{1,0:T(1,128)S(1)}, u32[]{:S(2)}, u32[]{:S(2)}) collective-permute-start(f32[1,128]{1,0:T(1,128)S(1)} %add.31), channel_id=1, source_target_pairs={{0,3},{1,2},{2,1},{3,0},{4,7},{5,6},{6,5},{7,4},{8,11},{9,10},{10,... | collective-permute-start | bytes 1544 | tf_op jit(solution)/shard_map/ppermute | solution.py:19

commit v2 on v1

--- a/solution.py
+++ b/solution.py
@@ -9,6 +9,7 @@
 
 
 GRANT = 12 << 20
+PARTS = 1
 LANES = 128
 VMEM = pl.BlockSpec(memory_space=pltpu.VMEM)
 HBM = pl.BlockSpec(memory_space=pltpu.HBM)
@@ -61,11 +62,32 @@
     return values * inverse, inverse
 
 
-def image_norm_kernel(raw_ref, b_ref, unit_ref, inv_ref):
-    unit, inverse = unit_parts(raw_ref[...])
-    b_ref[...] = unit.astype(jnp.bfloat16)
-    unit_ref[...] = unit
-    inv_ref[...] = jnp.broadcast_to(inverse, inv_ref.shape)
+def norm_kernel(raw_ref, *refs):
+    outs, (buf, sems) = refs[:-2], refs[-2:]
+    parts = sems.shape[0]
+    step = buf.shape[0] // parts
+    spans = [pl.ds(k * step, step) for k in range(parts)]
+    copies = [pltpu.make_async_copy(raw_ref.at[at], buf.at[at], sems.at[k]) for k, at in enumerate(spans)]
+    for copy in copies:
+        copy.start()
+    for copy, at in zip(copies, spans):
+        copy.wait()
+        unit, inverse = unit_parts(buf[at, :])
+        outs[0][at, :] = unit.astype(jnp.bfloat16)
+        if len(outs) > 1:
+            outs[1][at, :] = unit
+            outs[2][at, :] = jnp.broadcast_to(inverse, (step, LANES))
+
+
+def normed(raw, outs):
+    rows, width = raw.shape
+    return kernel_call(
+        norm_kernel,
+        outs,
+        (pltpu.with_memory_space_constraint(raw, pltpu.HBM),),
+        [pltpu.VMEM((rows, width), jnp.float32), pltpu.SemaphoreType.DMA((PARTS,))],
+        in_hbm=1,
+    )
 
 
 def text_parts_kernel(raw_ref, unit_ref, inv_ref):
@@ -164,7 +186,7 @@
     if n_row & (n_row - 1) or n_col & (n_col - 1) or n_col < 2:
         return lax.psum(value, ("row", "col"))[0, :1]
     flips = [1]
-    flips += [n_col << k | 1 for k in range(n_row.bit_length() - 1)]
+    flips += [n_col << k | 1 for k in reversed(range(n_row.bit_length() - 1))]
     flips += [1 << k | 1 for k in range(1, n_col.bit_length() - 1)]
     for flip in flips:
         other = moved(value, ("row", "col"), lambda i: i ^ flip)
@@ -196,10 +218,10 @@
 
     wide = jax.ShapeDtypeStruct((rows, width), f32)
     column = jax.ShapeDtypeStruct((rows, LANES), f32)
-    txt_b = unit_parts(text_embed)[0].astype(jnp.bfloat16)
+    half = jax.ShapeDtypeStruct((rows, width), jnp.bfloat16)
+    txt_b = normed(text_embed, half)
     txt_far = across(txt_b, cores)
-    half = jax.ShapeDtypeStruct((rows, width), jnp.bfloat16)
-    img_b, img_unit, img_inv = kernel_call(image_norm_kernel, (half, wide, column), (image_embed,))
+    img_b, img_unit, img_inv = normed(image_embed, (half, wide, column))
     txt_unit, txt_inv = kernel_call(text_parts_kernel, (wide, column), (text_embed,))
     img_far = across(img_b, cores)
     txt_near = partners(txt_b, cores)

time: 40.1 us -> 40.1 us (level)
  Pallas kernels: 5.5 us -> 7.83 us
  other arithmetic: 1.95 us -> 0.6 us
  starting transfers between devices: 14.1 us -> 13.1 us
    pallas_call x7 -> x8, Pallas kernels: 5.5 us -> 7.83 us  [kernel_call(): pl.pallas_call(body, out_shape=outs, in_specs=[HBM] * in_hbm + [VMEM] * (...]
    reduce_sum x1 -> x0, other arithmetic: 1.25 us -> none  [unit_parts(): jnp.sum(values * values, axis=1, keepdims=True) + 1e-06]
    ppermute x11, starting transfers between devices: 14.1 us -> 13.1 us  [moved(): return lax.ppermute(value, axis, [(i, target(i)) for i in range(count)])]
  transfers between devices with their start and end apart: 11 -> 11, of which waited for: 7 -> 7; matrix products, arithmetic and copies ran while one was open for 2% -> 2% of each run, Pallas kernels for 10% -> 13%
where the time goes in v2:
time: 40.1 us; the launch traced here: 39.9 us
  waiting for transfers between devices  16.2 us (40%)
  starting transfers between devices  13.1 us (33%)
  Pallas kernels  7.83 us (20%)
  between operations  2.04 us (5%)
  other arithmetic  0.6 us (1%)
    ppermute x11, waiting for transfers between devices, moved(): return lax.ppermute(value, axis, [(i, target(i)) for i in range(count)])  16.2 us
    ppermute x11, starting transfers between devices, moved(): return lax.ppermute(value, axis, [(i, target(i)) for i in range(count)])  13.1 us
    pallas_call x8, Pallas kernels, kernel_call(): pl.pallas_call(body, out_shape=outs, in_specs=[HBM] * in_hbm + [VMEM] * (...  7.83 us
  transfers between devices with their start and end apart: 11, of which 7 were waited for; matrix products, arithmetic and copies ran while one was open for 2% of the time, Pallas kernels for 13%

profile of v2, /device:TPU:0, one launch (start us, length us, event | category | flops | bytes accessed | tf_op | source)
XLA Modules:
  0.0 39.9 jit_solution(1543815621345549261)
XLA Ops:
  0.6 1.2 %shard_map.67.txt_ref.own_ref = bf16[128,1152]{1,0:T(8,128)(2,1)S(1)} custom-call(f32[128,1152]{1,0:T(8,128)} %raw_ref.5), custom_call_target="tpu_custom_call" | custom-call | tf_op jit(solution)/shard_map/pallas_call | solution.py:24
  1.9 2.5 %collective-permute-start.2 = (bf16[128,1152]{1,0:T(8,128)(2,1)S(1)}, bf16[128,1152]{1,0:T(8,128)(2,1)S(1)}, u32[]{:S(2)}, u32[]{:S(2)}) collective-permute-start(bf16[128,1152]{1,0:T(8,128)(2,1)S(1)} %shard_map.67.txt_ref.own_ref), channel_id=1, source_target_pairs={{0,3},{1,2},{2,1},{3,0},{4,7},{5,6},{6,5},{7,4},{8,11},{9,10},{10,... | collective-permute-start | bytes 884744 | tf_op jit(solution)/shard_map/ppermute | solution.py:20
  4.3 1.2 %shard_map.68 = (bf16[128,1152]{1,0:T(8,128)(2,1)S(1)}, f32[128,1152]{1,0:T(8,128)S(1)}, f32[128,128]{1,0:T(8,128)S(1)}) custom-call(f32[128,1152]{1,0:T(8,128)} %raw_ref.4), custom_call_target="tpu_custom_call" | custom-call | tf_op jit(solution)/shard_map/pallas_call | solution.py:24
  5.6 0.1 collective-permute-start.9
  5.7 0.7 %collective-permute-start = (bf16[128,1152]{1,0:T(8,128)(2,1)S(1)}, bf16[128,1152]{1,0:T(8,128)(2,1)S(1)}, u32[]{:S(2)}, u32[]{:S(2)}) collective-permute-start(bf16[128,1152]{1,0:T(8,128)(2,1)S(1)} %shard_map.67.txt_ref.own_ref), channel_id=1, source_target_pairs={{0,1},{1,0},{2,3},{3,2},{4,5},{5,4},{6,7},{7,6},{8,9},{9,8},{10,11... | collective-permute-start | bytes 884744 | tf_op jit(solution)/shard_map/ppermute | solution.py:20
  6.4 0.1 collective-permute-start.1
  6.5 5.3 %collective-permute-done.2.refs_2_.refs_0_ = bf16[128,1152]{1,0:T(8,128)(2,1)S(1)} collective-permute-done((bf16[128,1152]{1,0:T(8,128)(2,1)S(1)}, bf16[128,1152]{1,0:T(8,128)(2,1)S(1)}, u32[]{:S(2)}, u32[]{:S(2)}) %collective-permute-start.2) | collective-permute-done | bytes 294944 | tf_op jit(solution)/shard_map/ppermute | solution.py:20
  11.7 1.1 %collective-permute-start.8 = (bf16[128,1152]{1,0:T(8,128)(2,1)S(1)}, bf16[128,1152]{1,0:T(8,128)(2,1)S(1)}, u32[]{:S(2)}, u32[]{:S(2)}) collective-permute-start(bf16[128,1152]{1,0:T(8,128)(2,1)S(1)} %collective-permute-done.2.refs_2_.refs_0_), channel_id=1, source_target_pairs={{0,1},{1,0},{2,3},{3,2},{4,5},{5,4},{6,7},{7,6},{8,9},{9,8},{10,11... | collective-permute-start | bytes 884744 | tf_op jit(solution)/shard_map/ppermute | solution.py:20
  12.9 5.2 %collective-permute-done.9.refs_0_ = bf16[128,1152]{1,0:T(8,128)(2,1)S(1)} collective-permute-done((bf16[128,1152]{1,0:T(8,128)(2,1)S(1)}, bf16[128,1152]{1,0:T(8,128)(2,1)S(1)}, u32[]{:S(2)}, u32[]{:S(2)}) %collective-permute-start.9) | collective-permute-done | bytes 294944 | tf_op jit(solution)/shard_map/ppermute | solution.py:20
  18.1 0.1 collective-permute-start.10
  19.5 0.1 maximum_bitcast_fusion
  19.6 0.0 collective-permute-done.refs_0_
  19.6 0.0 collective-permute-done.1.refs_1_
  19.6 0.1 broadcast_in_dim.8.par_ref
  19.6 1.2 %shard_map.69 = (f32[128,1152]{1,0:T(8,128)S(1)}, f32[128,1152]{1,0:T(8,128)S(1)}, f32[1,128]{1,0:T(1,128)S(1)}) custom-call(f32[2,128]{1,0:T(2,128)S(1)} %broadcast_in_dim.8.par_ref, bf16[128,1152]{1,0:T(8,128)(2,1)S(1)} %shard_map.67.txt_ref.own_ref, bf16[128,1152]{1,0:T(8,128)(2,1)S(1)} %get-tuple-element.11.img_ref.refs_0_.own_ref, ...), custom_call_target="tpu_custom_call" | custom-call | flops 301989888 | tf_op jit(solution)/shard_map/pallas_call | solution.py:24
  20.8 0.0 copy-start
  20.9 0.5 %shard_map.70 = f32[1,128]{1,0:T(1,128)S(1)} custom-call(f32[2,128]{1,0:T(2,128)S(1)} %broadcast_in_dim.8.par_ref, f32[1,128]{1,0:T(1,128)S(1)} %get-tuple-element.12.near_ref, bf16[128,1152]{1,0:T(8,128)(2,1)S(1)} %get-tuple-element.11.img_ref.refs_0_.own_ref, bf16[128,1152]{1,0:T(8,128)(2,1)S(1)} %collective-permute-done.1.refs_1_, ...), custom_call_target="tpu_custom_call" | custom-call | flops 75497472 | tf_op jit(solution)/shard_map/pallas_call | solution.py:24
  21.3 0.4 %collective-permute-start.3 = (f32[1,128]{1,0:T(1,128)S(1)}, f32[1,128]{1,0:T(1,128)S(1)}, u32[]{:S(2)}, u32[]{:S(2)}) collective-permute-start(f32[1,128]{1,0:T(1,128)S(1)} %shard_map.70), channel_id=1, source_target_pairs={{0,1},{1,0},{2,3},{3,2},{4,5},{5,4},{6,7},{7,6},{8,9},{9,8},{10,11... | collective-permute-start | bytes 1544 | tf_op jit(solution)/shard_map/ppermute | solution.py:20
  21.7 0.8 %collective-permute-done.3 = f32[1,128]{1,0:T(1,128)S(1)} collective-permute-done((f32[1,128]{1,0:T(1,128)S(1)}, f32[1,128]{1,0:T(1,128)S(1)}, u32[]{:S(2)}, u32[]{:S(2)}) %collective-permute-start.3) | collective-permute-done | bytes 544 | tf_op jit(solution)/shard_map/ppermute | solution.py:20
  22.6 3.5 %collective-permute-start.4 = (f32[1,128]{1,0:T(1,128)S(1)}, f32[1,128]{1,0:T(1,128)S(1)}, u32[]{:S(2)}, u32[]{:S(2)}) collective-permute-start(f32[1,128]{1,0:T(1,128)S(1)} %add.15), channel_id=1, source_target_pairs={{0,17},{1,16},{2,19},{3,18},{4,21},{5,20},{6,23},{7,22},{8,25},{9,... | collective-permute-start | bytes 1544 | tf_op jit(solution)/shard_map/ppermute | solution.py:20
  26.0 1.3 %collective-permute-done.4 = f32[1,128]{1,0:T(1,128)S(1)} collective-permute-done((f32[1,128]{1,0:T(1,128)S(1)}, f32[1,128]{1,0:T(1,128)S(1)}, u32[]{:S(2)}, u32[]{:S(2)}) %collective-permute-start.4) | collective-permute-done | bytes 544 | tf_op jit(solution)/shard_map/ppermute | solution.py:20
  27.3 1.6 %collective-permute-start.5 = (f32[1,128]{1,0:T(1,128)S(1)}, f32[1,128]{1,0:T(1,128)S(1)}, u32[]{:S(2)}, u32[]{:S(2)}) collective-permute-start(f32[1,128]{1,0:T(1,128)S(1)} %add.16), channel_id=1, source_target_pairs={{0,9},{1,8},{2,11},{3,10},{4,13},{5,12},{6,15},{7,14},{8,1},{9,0},... | collective-permute-start | bytes 1544 | tf_op jit(solution)/shard_map/ppermute | solution.py:20
  28.9 1.4 %collective-permute-done.5 = f32[1,128]{1,0:T(1,128)S(1)} collective-permute-done((f32[1,128]{1,0:T(1,128)S(1)}, f32[1,128]{1,0:T(1,128)S(1)}, u32[]{:S(2)}, u32[]{:S(2)}) %collective-permute-start.5) | collective-permute-done | bytes 544 | tf_op jit(solution)/shard_map/ppermute | solution.py:20
  30.3 1.5 %collective-permute-start.6 = (f32[1,128]{1,0:T(1,128)S(1)}, f32[1,128]{1,0:T(1,128)S(1)}, u32[]{:S(2)}, u32[]{:S(2)}) collective-permute-start(f32[1,128]{1,0:T(1,128)S(1)} %add.17), channel_id=1, source_target_pairs={{0,5},{1,4},{2,7},{3,6},{4,1},{5,0},{6,3},{7,2},{8,13},{9,12},{10,... | collective-permute-start | bytes 1544 | tf_op jit(solution)/shard_map/ppermute | solution.py:20
  31.9 0.1 shard_map.73
  32.0 1.3 %collective-permute-done.6 = f32[1,128]{1,0:T(1,128)S(1)} collective-permute-done((f32[1,128]{1,0:T(1,128)S(1)}, f32[1,128]{1,0:T(1,128)S(1)}, u32[]{:S(2)}, u32[]{:S(2)}) %collective-permute-start.6) | collective-permute-done | bytes 544 | tf_op jit(solution)/shard_map/ppermute | solution.py:20
  33.3 1.5 %collective-permute-start.7 = (f32[1,128]{1,0:T(1,128)S(1)}, f32[1,128]{1,0:T(1,128)S(1)}, u32[]{:S(2)}, u32[]{:S(2)}) collective-permute-start(f32[1,128]{1,0:T(1,128)S(1)} %add.18), channel_id=1, source_target_pairs={{0,3},{1,2},{2,1},{3,0},{4,7},{5,6},{6,5},{7,4},{8,11},{9,10},{10,... | collective-permute-start | bytes 1544 | tf_op jit(solution)/shard_map/ppermute | solution.py:20
  34.9 0.5 %shard_map.72.carry_ref = f32[128,1152]{1,0:T(8,128)S(1)} custom-call(f32[2,128]{1,0:T(2,128)S(1)} %broadcast_in_dim.8.par_ref, bf16[128,1152]{1,0:T(8,128)(2,1)S(1)} %shard_map.67.txt_ref.own_ref, f32[128,1152]{1,0:T(8,128)S(1)} %get-tuple-element.16.carry_ref, bf16[128,1152]{1,0:T(8,128)(2,1)S(1)} %collective-permute-done.9.refs_0_), custom_call_target="tpu_custom_call" | custom-call | flops 75497472 | tf_op jit(solution)/shard_map/pallas_call | solution.py:24
  35.4 0.9 %collective-permute-done.7 = f32[1,128]{1,0:T(1,128)S(1)} collective-permute-done((f32[1,128]{1,0:T(1,128)S(1)}, f32[1,128]{1,0:T(1,128)S(1)}, u32[]{:S(2)}, u32[]{:S(2)}) %collective-permute-start.7) | collective-permute-done | bytes 544 | tf_op jit(solution)/shard_map/ppermute | solution.py:20
  36.3 0.5 %add.19 = f32[1,128]{1,0:T(1,128)} add(f32[1,128]{1,0:T(1,128)S(1)} %add.18, f32[1,128]{1,0:T(1,128)S(1)} %collective-permute-done.7) | non-fusion elementwise | flops 128 | bytes 1536 | tf_op jit(solution)/shard_map/add | solution.py:193
  36.8 1.6 %shard_map.71 = f32[128,1152]{1,0:T(8,128)} custom-call(f32[2,128]{1,0:T(2,128)S(1)} %broadcast_in_dim.8.par_ref, bf16[128,1152]{1,0:T(8,128)(2,1)S(1)} %get-tuple-element.11.img_ref.refs_0_.own_ref, f32[128,1152]{1,0:T(8,128)S(1)} %get-tuple-element.13.carry_ref, f32[128,1152]{1,0:T(8,128)S(1)} %get-tuple-element.14.unit_ref, ...), custom_call_target="tpu_custom_call" | custom-call | flops 150994944 | tf_op jit(solution)/shard_map/pallas_call | solution.py:24
  38.4 1.4 %shard_map.74 = f32[128,1152]{1,0:T(8,128)} custom-call(f32[2,128]{1,0:T(2,128)S(1)} %broadcast_in_dim.8.par_ref, bf16[128,1152]{1,0:T(8,128)(2,1)S(1)} %shard_map.67.txt_ref.own_ref, f32[128,1152]{1,0:T(8,128)S(1)} %shard_map.72.carry_ref, f32[128,1152]{1,0:T(8,128)S(1)} %get-tuple-element.17.unit_ref, f32[128,128]{1,0:T(8,128)S(1)} %get-tuple-element.18.inv_ref, ...), custom_call_target="tpu_custom_call" | custom-call | flops 75497472 | tf_op jit(solution)/shard_map/pallas_call | solution.py:24
  (7 shorter events, 0.0 us)
Async XLA Ops:
  1.9 9.9 %collective-permute-start.2 = (bf16[128,1152]{1,0:T(8,128)(2,1)S(1)}, bf16[128,1152]{1,0:T(8,128)(2,1)S(1)}, u32[]{:S(2)}, u32[]{:S(2)}) collective-permute-start(bf16[128,1152]{1,0:T(8,128)(2,1)S(1)} %shard_map.67.txt_ref.own_ref), channel_id=1, source_target_pairs={{0,3},{1,2},{2,1},{3,0},{4,7},{5,6},{6,5},{7,4},{8,11},{9,10},{10,... | collective-permute-start | bytes 884744 | tf_op jit(solution)/shard_map/ppermute | solution.py:20
  5.6 12.5 %collective-permute-start.9 = (bf16[128,1152]{1,0:T(8,128)(2,1)S(1)}, bf16[128,1152]{1,0:T(8,128)(2,1)S(1)}, u32[]{:S(2)}, u32[]{:S(2)}) collective-permute-start(bf16[128,1152]{1,0:T(8,128)(2,1)S(1)} %get-tuple-element.11.img_ref.refs_0_.own_ref), channel_id=1, source_target_pairs={{0,3},{1,2},{2,1},{3,0},{4,7},{5,6},{6,5},{7,4},{8,11},{9,10},{10,... | collective-permute-start | bytes 884744 | tf_op jit(solution)/shard_map/ppermute | solution.py:20
  5.7 13.9 %collective-permute-start = (bf16[128,1152]{1,0:T(8,128)(2,1)S(1)}, bf16[128,1152]{1,0:T(8,128)(2,1)S(1)}, u32[]{:S(2)}, u32[]{:S(2)}) collective-permute-start(bf16[128,1152]{1,0:T(8,128)(2,1)S(1)} %shard_map.67.txt_ref.own_ref), channel_id=1, source_target_pairs={{0,1},{1,0},{2,3},{3,2},{4,5},{5,4},{6,7},{7,6},{8,9},{9,8},{10,11... | collective-permute-start | bytes 884744 | tf_op jit(solution)/shard_map/ppermute | solution.py:20
  6.4 13.2 %collective-permute-start.1 = (bf16[128,1152]{1,0:T(8,128)(2,1)S(1)}, bf16[128,1152]{1,0:T(8,128)(2,1)S(1)}, u32[]{:S(2)}, u32[]{:S(2)}) collective-permute-start(bf16[128,1152]{1,0:T(8,128)(2,1)S(1)} %get-tuple-element.11.img_ref.refs_0_.own_ref), channel_id=1, source_target_pairs={{0,1},{1,0},{2,3},{3,2},{4,5},{5,4},{6,7},{7,6},{8,9},{9,8},{10,11... | collective-permute-start | bytes 884744 | tf_op jit(solution)/shard_map/ppermute | solution.py:20
  11.7 25.1 %collective-permute-start.8 = (bf16[128,1152]{1,0:T(8,128)(2,1)S(1)}, bf16[128,1152]{1,0:T(8,128)(2,1)S(1)}, u32[]{:S(2)}, u32[]{:S(2)}) collective-permute-start(bf16[128,1152]{1,0:T(8,128)(2,1)S(1)} %collective-permute-done.2.refs_2_.refs_0_), channel_id=1, source_target_pairs={{0,1},{1,0},{2,3},{3,2},{4,5},{5,4},{6,7},{7,6},{8,9},{9,8},{10,11... | collective-permute-start | bytes 884744 | tf_op jit(solution)/shard_map/ppermute | solution.py:20
  18.1 20.4 %collective-permute-start.10 = (bf16[128,1152]{1,0:T(8,128)(2,1)S(1)}, bf16[128,1152]{1,0:T(8,128)(2,1)S(1)}, u32[]{:S(2)}, u32[]{:S(2)}) collective-permute-start(bf16[128,1152]{1,0:T(8,128)(2,1)S(1)} %collective-permute-done.9.refs_0_), channel_id=1, source_target_pairs={{0,1},{1,0},{2,3},{3,2},{4,5},{5,4},{6,7},{7,6},{8,9},{9,8},{10,11... | collective-permute-start | bytes 884744 | tf_op jit(solution)/shard_map/ppermute | solution.py:20
  20.8 11.0 %copy-start = (f32[128,1152]{1,0:T(8,128)S(1)}, f32[128,1152]{1,0:T(8,128)}, u32[]{:S(2)}) copy-start(f32[128,1152]{1,0:T(8,128)} %raw_ref.5) | copy-start | bytes 1769476
  21.3 1.2 %collective-permute-start.3 = (f32[1,128]{1,0:T(1,128)S(1)}, f32[1,128]{1,0:T(1,128)S(1)}, u32[]{:S(2)}, u32[]{:S(2)}) collective-permute-start(f32[1,128]{1,0:T(1,128)S(1)} %shard_map.70), channel_id=1, source_target_pairs={{0,1},{1,0},{2,3},{3,2},{4,5},{5,4},{6,7},{7,6},{8,9},{9,8},{10,11... | collective-permute-start | bytes 1544 | tf_op jit(solution)/shard_map/ppermute | solution.py:20
  22.6 4.8 %collective-permute-start.4 = (f32[1,128]{1,0:T(1,128)S(1)}, f32[1,128]{1,0:T(1,128)S(1)}, u32[]{:S(2)}, u32[]{:S(2)}) collective-permute-start(f32[1,128]{1,0:T(1,128)S(1)} %add.15), channel_id=1, source_target_pairs={{0,17},{1,16},{2,19},{3,18},{4,21},{5,20},{6,23},{7,22},{8,25},{9,... | collective-permute-start | bytes 1544 | tf_op jit(solution)/shard_map/ppermute | solution.py:20
  27.3 3.0 %collective-permute-start.5 = (f32[1,128]{1,0:T(1,128)S(1)}, f32[1,128]{1,0:T(1,128)S(1)}, u32[]{:S(2)}, u32[]{:S(2)}) collective-permute-start(f32[1,128]{1,0:T(1,128)S(1)} %add.16), channel_id=1, source_target_pairs={{0,9},{1,8},{2,11},{3,10},{4,13},{5,12},{6,15},{7,14},{8,1},{9,0},... | collective-permute-start | bytes 1544 | tf_op jit(solution)/shard_map/ppermute | solution.py:20
  30.3 3.0 %collective-permute-start.6 = (f32[1,128]{1,0:T(1,128)S(1)}, f32[1,128]{1,0:T(1,128)S(1)}, u32[]{:S(2)}, u32[]{:S(2)}) collective-permute-start(f32[1,128]{1,0:T(1,128)S(1)} %add.17), channel_id=1, source_target_pairs={{0,5},{1,4},{2,7},{3,6},{4,1},{5,0},{6,3},{7,2},{8,13},{9,12},{10,... | collective-permute-start | bytes 1544 | tf_op jit(solution)/shard_map/ppermute | solution.py:20
  33.3 3.0 %collective-permute-start.7 = (f32[1,128]{1,0:T(1,128)S(1)}, f32[1,128]{1,0:T(1,128)S(1)}, u32[]{:S(2)}, u32[]{:S(2)}) collective-permute-start(f32[1,128]{1,0:T(1,128)S(1)} %add.18), channel_id=1, source_target_pairs={{0,3},{1,2},{2,1},{3,0},{4,7},{5,6},{6,5},{7,4},{8,11},{9,10},{10,... | collective-permute-start | bytes 1544 | tf_op jit(solution)/shard_map/ppermute | solution.py:20

commit v3 on v2

--- a/solution.py
+++ b/solution.py
@@ -90,20 +90,28 @@
     )
 
 
-def text_parts_kernel(raw_ref, unit_ref, inv_ref):
-    unit, inverse = unit_parts(raw_ref[...])
+def parts_kernel(raw_ref, unit_ref, inv_ref, buf, sem):
+    copy = pltpu.make_async_copy(raw_ref, buf, sem)
+    copy.start()
+    copy.wait()
+    unit, inverse = unit_parts(buf[...])
     unit_ref[...] = unit
     inv_ref[...] = jnp.broadcast_to(inverse, inv_ref.shape)
+
+
+def copy_kernel(from_ref, to_ref):
+    to_ref[...] = from_ref[...]
 
 
 def near_kernel(count, par_ref, txt_ref, img_ref, *refs):
     texts = (txt_ref,) + refs[: count - 1]
     images = (img_ref,) + refs[count - 1 : 2 * count - 2]
-    img_sum_ref, txt_sum_ref, loss_ref = refs[2 * count - 2 :]
+    img_sum_ref, txt_sum_ref, pair_ref, loss_ref = refs[2 * count - 2 :]
     rows = txt_ref.shape[0]
     img_sum = txt_sum = loss = None
     for j in range(count):
         sign = eye_signs(rows) if j == 0 else -1.0
+        pair_ref[pl.ds(j * rows, rows), :] = images[j][...]
         arg = -sign * logits_of(par_ref, img_ref[...], texts[j][...])
         term = dot_n(weights(arg, sign), texts[j][...])
         img_sum = term if j == 0 else img_sum + term
@@ -114,18 +122,16 @@
         loss = part if j == 0 else loss + part
     img_sum_ref[...] = img_sum
     txt_sum_ref[...] = txt_sum
-    loss_ref[...] = jnp.broadcast_to(jnp.sum(loss, axis=1, keepdims=True), loss_ref.shape)
-
-
-def far_loss_kernel(n_img, pairs, par_ref, near_ref, *refs):
-    images, texts, loss_ref = refs[:n_img], refs[n_img:-1], refs[-1]
-    loss = None
-    for image in images:
-        for text in texts:
-            part = jnp.sum(softplus(logits_of(par_ref, image[...], text[...])), axis=0, keepdims=True)
-            loss = part if loss is None else loss + part
-    total = near_ref[...] + jnp.broadcast_to(jnp.sum(loss, axis=1, keepdims=True), loss_ref.shape)
-    loss_ref[...] = total / pairs
+    loss_ref[...] = loss
+
+
+def far_loss_kernel(pairs, par_ref, near_ref, pair_ref, *refs):
+    total = near_ref[...]
+    for text in refs[:-1]:
+        part = jnp.sum(softplus(logits_of(par_ref, text[...], pair_ref[...])), axis=0, keepdims=True)
+        for j in range(part.shape[1] // LANES):
+            total = total + part[:, j * LANES : (j + 1) * LANES]
+    refs[-1][...] = jnp.broadcast_to(jnp.sum(total, axis=1, keepdims=True) / pairs, refs[-1].shape)
 
 
 def sum_kernel(par_ref, own_ref, carry_ref, *refs):
@@ -184,7 +190,7 @@
 def summed(value):
     n_row, n_col = lax.axis_size("row"), lax.axis_size("col")
     if n_row & (n_row - 1) or n_col & (n_col - 1) or n_col < 2:
-        return lax.psum(value, ("row", "col"))[0, :1]
+        return jnp.sum(lax.psum(value, ("row", "col")), axis=1)
     flips = [1]
     flips += [n_col << k | 1 for k in reversed(range(n_row.bit_length() - 1))]
     flips += [1 << k | 1 for k in range(1, n_col.bit_length() - 1)]
@@ -222,23 +228,31 @@
     txt_b = normed(text_embed, half)
     txt_far = across(txt_b, cores)
     img_b, img_unit, img_inv = normed(image_embed, (half, wide, column))
-    txt_unit, txt_inv = kernel_call(text_parts_kernel, (wide, column), (text_embed,))
+    txt_unit, txt_inv = kernel_call(
+        parts_kernel,
+        (wide, column),
+        (pltpu.with_memory_space_constraint(text_embed, pltpu.HBM),),
+        [pltpu.VMEM((rows, width), f32), pltpu.SemaphoreType.DMA],
+        in_hbm=1,
+    )
     img_far = across(img_b, cores)
     txt_near = partners(txt_b, cores)
     img_near = partners(img_b, cores)
     terms = jax.ShapeDtypeStruct((1, LANES), f32)
-    img_sum, txt_sum, loss = kernel_call(
+    pair = jax.ShapeDtypeStruct((cores * rows, width), jnp.bfloat16)
+    img_sum, txt_sum, pair, loss = kernel_call(
         functools.partial(near_kernel, cores),
-        (wide, wide, terms),
+        (wide, wide, pair, terms),
         (params, txt_b, img_b, *txt_near, *img_near),
         flops=4 * flops * cores,
     )
+    params = kernel_call(copy_kernel, jax.ShapeDtypeStruct(params.shape, f32), (params,))
     if txt_far:
         txt_rest = [other for block in txt_far for other in partners(block, cores)]
         loss = kernel_call(
-            functools.partial(far_loss_kernel, cores, rows * n_row * n_col),
+            functools.partial(far_loss_kernel, rows * n_row * n_col),
             terms,
-            (params, loss, img_b, *img_near, *txt_far),
+            (params, loss, pair, *txt_far),
             flops=flops * cores * len(txt_far),
         )
         img_rest = [other for block in img_far for other in partners(block, cores)]

time: 40.1 us -> 40.1 us (level)
  waiting for transfers between devices: 16.2 us -> 15.1 us
  Pallas kernels: 7.83 us -> 8.92 us
    pallas_call x8 -> x9, Pallas kernels: 7.83 us -> 8.92 us  [kernel_call(): pl.pallas_call(body, out_shape=outs, in_specs=[HBM] * in_hbm + [VMEM] * (...]
    ppermute x11, waiting for transfers between devices: 16.2 us -> 15.1 us  [moved(): return lax.ppermute(value, axis, [(i, target(i)) for i in range(count)])]
  transfers between devices with their start and end apart: 11 -> 11, of which waited for: 7 -> 7; matrix products, arithmetic and copies ran while one was open for 2% -> 2% of each run, Pallas kernels for 13% -> 16%
where the time goes in v3:
time: 40.1 us; the launch traced here: 39.9 us
  waiting for transfers between devices  15.1 us (38%)
  starting transfers between devices  13.1 us (33%)
  Pallas kernels  8.92 us (22%)
  between operations  2.03 us (5%)
  other arithmetic  0.6 us (1%)
    ppermute x11, waiting for transfers between devices, moved(): return lax.ppermute(value, axis, [(i, target(i)) for i in range(count)])  15.1 us
    ppermute x11, starting transfers between devices, moved(): return lax.ppermute(value, axis, [(i, target(i)) for i in range(count)])  13.1 us
    pallas_call x9, Pallas kernels, kernel_call(): pl.pallas_call(body, out_shape=outs, in_specs=[HBM] * in_hbm + [VMEM] * (...  8.92 us
  transfers between devices with their start and end apart: 11, of which 7 were waited for; matrix products, arithmetic and copies ran while one was open for 2% of the time, Pallas kernels for 16%

profile of v3, /device:TPU:0, one launch (start us, length us, event | category | flops | bytes accessed | tf_op | source)
XLA Modules:
  0.0 39.9 jit_solution(1183888484098700929)
XLA Ops:
  0.6 1.2 %shard_map.68.txt_ref.own_ref = bf16[128,1152]{1,0:T(8,128)(2,1)S(1)} custom-call(f32[128,1152]{1,0:T(8,128)} %raw_ref.5), custom_call_target="tpu_custom_call" | custom-call | tf_op jit(solution)/shard_map/pallas_call | solution.py:24
  1.9 2.5 %collective-permute-start.2 = (bf16[128,1152]{1,0:T(8,128)(2,1)S(1)}, bf16[128,1152]{1,0:T(8,128)(2,1)S(1)}, u32[]{:S(2)}, u32[]{:S(2)}) collective-permute-start(bf16[128,1152]{1,0:T(8,128)(2,1)S(1)} %shard_map.68.txt_ref.own_ref), channel_id=1, source_target_pairs={{0,3},{1,2},{2,1},{3,0},{4,7},{5,6},{6,5},{7,4},{8,11},{9,10},{10,... | collective-permute-start | bytes 884744 | tf_op jit(solution)/shard_map/ppermute | solution.py:20
  4.3 1.2 %shard_map.69 = (bf16[128,1152]{1,0:T(8,128)(2,1)S(1)}, f32[128,1152]{1,0:T(8,128)S(1)}, f32[128,128]{1,0:T(8,128)S(1)}) custom-call(f32[128,1152]{1,0:T(8,128)} %raw_ref.4), custom_call_target="tpu_custom_call" | custom-call | tf_op jit(solution)/shard_map/pallas_call | solution.py:24
  5.6 0.1 collective-permute-start.9
  5.7 0.7 %collective-permute-start = (bf16[128,1152]{1,0:T(8,128)(2,1)S(1)}, bf16[128,1152]{1,0:T(8,128)(2,1)S(1)}, u32[]{:S(2)}, u32[]{:S(2)}) collective-permute-start(bf16[128,1152]{1,0:T(8,128)(2,1)S(1)} %shard_map.68.txt_ref.own_ref), channel_id=1, source_target_pairs={{0,1},{1,0},{2,3},{3,2},{4,5},{5,4},{6,7},{7,6},{8,9},{9,8},{10,11... | collective-permute-start | bytes 884744 | tf_op jit(solution)/shard_map/ppermute | solution.py:20
  6.4 0.1 collective-permute-start.1
  6.5 5.3 %collective-permute-done.2.refs_0_ = bf16[128,1152]{1,0:T(8,128)(2,1)S(1)} collective-permute-done((bf16[128,1152]{1,0:T(8,128)(2,1)S(1)}, bf16[128,1152]{1,0:T(8,128)(2,1)S(1)}, u32[]{:S(2)}, u32[]{:S(2)}) %collective-permute-start.2) | collective-permute-done | bytes 294944 | tf_op jit(solution)/shard_map/ppermute | solution.py:20
  11.7 1.1 %collective-permute-start.8 = (bf16[128,1152]{1,0:T(8,128)(2,1)S(1)}, bf16[128,1152]{1,0:T(8,128)(2,1)S(1)}, u32[]{:S(2)}, u32[]{:S(2)}) collective-permute-start(bf16[128,1152]{1,0:T(8,128)(2,1)S(1)} %collective-permute-done.2.refs_0_), channel_id=1, source_target_pairs={{0,1},{1,0},{2,3},{3,2},{4,5},{5,4},{6,7},{7,6},{8,9},{9,8},{10,11... | collective-permute-start | bytes 884744 | tf_op jit(solution)/shard_map/ppermute | solution.py:20
  12.9 5.2 %collective-permute-done.9.refs_0_ = bf16[128,1152]{1,0:T(8,128)(2,1)S(1)} collective-permute-done((bf16[128,1152]{1,0:T(8,128)(2,1)S(1)}, bf16[128,1152]{1,0:T(8,128)(2,1)S(1)}, u32[]{:S(2)}, u32[]{:S(2)}) %collective-permute-start.9) | collective-permute-done | bytes 294944 | tf_op jit(solution)/shard_map/ppermute | solution.py:20
  18.1 0.1 collective-permute-start.10
  19.5 0.1 maximum_bitcast_fusion
  19.6 0.1 broadcast_in_dim.8.from_ref.par_ref
  19.6 0.0 collective-permute-done.refs_0_
  19.6 0.0 collective-permute-done.1.refs_1_
  19.6 1.2 %shard_map.70 = (f32[128,1152]{1,0:T(8,128)S(1)}, f32[128,1152]{1,0:T(8,128)S(1)}, bf16[256,1152]{1,0:T(8,128)(2,1)S(1)}, f32[1,128]{1,0:T(1,128)S(1)}) custom-call(f32[2,128]{1,0:T(2,128)S(1)} %broadcast_in_dim.8.from_ref.par_ref, bf16[128,1152]{1,0:T(8,128)(2,1)S(1)} %shard_map.68.txt_ref.own_ref, bf16[128,1152]{1,0:T(8,128)(2,1)S(1)} %get-tuple-element.12.img_ref.own_ref, ...), custom_call_target="tpu_custom_call" | custom-call | flops 301989888 | tf_op jit(solution)/shard_map/pallas_call | solution.py:24
  20.9 0.5 %shard_map.71 = f32[1,128]{1,0:T(1,128)S(1)} custom-call(f32[2,128]{1,0:T(2,128)S(1)} %shard_map.67.par_ref, f32[1,128]{1,0:T(1,128)S(1)} %get-tuple-element.13.near_ref, bf16[256,1152]{1,0:T(8,128)(2,1)S(1)} %get-tuple-element.14.pair_ref, bf16[128,1152]{1,0:T(8,128)(2,1)S(1)} %collective-permute-done.2.refs_0_), custom_call_target="tpu_custom_call" | custom-call | flops 75497472 | tf_op jit(solution)/shard_map/pallas_call | solution.py:24
  21.3 0.4 %collective-permute-start.3 = (f32[1,128]{1,0:T(1,128)S(1)}, f32[1,128]{1,0:T(1,128)S(1)}, u32[]{:S(2)}, u32[]{:S(2)}) collective-permute-start(f32[1,128]{1,0:T(1,128)S(1)} %shard_map.71), channel_id=1, source_target_pairs={{0,1},{1,0},{2,3},{3,2},{4,5},{5,4},{6,7},{7,6},{8,9},{9,8},{10,11... | collective-permute-start | bytes 1544 | tf_op jit(solution)/shard_map/ppermute | solution.py:20
  21.8 0.8 %collective-permute-done.3 = f32[1,128]{1,0:T(1,128)S(1)} collective-permute-done((f32[1,128]{1,0:T(1,128)S(1)}, f32[1,128]{1,0:T(1,128)S(1)}, u32[]{:S(2)}, u32[]{:S(2)}) %collective-permute-start.3) | collective-permute-done | bytes 544 | tf_op jit(solution)/shard_map/ppermute | solution.py:20
  22.6 3.5 %collective-permute-start.4 = (f32[1,128]{1,0:T(1,128)S(1)}, f32[1,128]{1,0:T(1,128)S(1)}, u32[]{:S(2)}, u32[]{:S(2)}) collective-permute-start(f32[1,128]{1,0:T(1,128)S(1)} %add.15), channel_id=1, source_target_pairs={{0,17},{1,16},{2,19},{3,18},{4,21},{5,20},{6,23},{7,22},{8,25},{9,... | collective-permute-start | bytes 1544 | tf_op jit(solution)/shard_map/ppermute | solution.py:20
  26.1 1.3 %collective-permute-done.4 = f32[1,128]{1,0:T(1,128)S(1)} collective-permute-done((f32[1,128]{1,0:T(1,128)S(1)}, f32[1,128]{1,0:T(1,128)S(1)}, u32[]{:S(2)}, u32[]{:S(2)}) %collective-permute-start.4) | collective-permute-done | bytes 544 | tf_op jit(solution)/shard_map/ppermute | solution.py:20
  27.4 1.6 %collective-permute-start.5 = (f32[1,128]{1,0:T(1,128)S(1)}, f32[1,128]{1,0:T(1,128)S(1)}, u32[]{:S(2)}, u32[]{:S(2)}) collective-permute-start(f32[1,128]{1,0:T(1,128)S(1)} %add.16), channel_id=1, source_target_pairs={{0,9},{1,8},{2,11},{3,10},{4,13},{5,12},{6,15},{7,14},{8,1},{9,0},... | collective-permute-start | bytes 1544 | tf_op jit(solution)/shard_map/ppermute | solution.py:20
  28.9 1.4 %collective-permute-done.5 = f32[1,128]{1,0:T(1,128)S(1)} collective-permute-done((f32[1,128]{1,0:T(1,128)S(1)}, f32[1,128]{1,0:T(1,128)S(1)}, u32[]{:S(2)}, u32[]{:S(2)}) %collective-permute-start.5) | collective-permute-done | bytes 544 | tf_op jit(solution)/shard_map/ppermute | solution.py:20
  30.4 1.5 %collective-permute-start.6 = (f32[1,128]{1,0:T(1,128)S(1)}, f32[1,128]{1,0:T(1,128)S(1)}, u32[]{:S(2)}, u32[]{:S(2)}) collective-permute-start(f32[1,128]{1,0:T(1,128)S(1)} %add.17), channel_id=1, source_target_pairs={{0,5},{1,4},{2,7},{3,6},{4,1},{5,0},{6,3},{7,2},{8,13},{9,12},{10,... | collective-permute-start | bytes 1544 | tf_op jit(solution)/shard_map/ppermute | solution.py:20
  31.9 1.2 %shard_map.74 = (f32[128,1152]{1,0:T(8,128)S(1)}, f32[128,128]{1,0:T(8,128)S(1)}) custom-call(f32[128,1152]{1,0:T(8,128)} %raw_ref.5), custom_call_target="tpu_custom_call" | custom-call | tf_op jit(solution)/shard_map/pallas_call | solution.py:24
  33.1 0.2 collective-permute-done.6
  33.4 1.5 %collective-permute-start.7 = (f32[1,128]{1,0:T(1,128)S(1)}, f32[1,128]{1,0:T(1,128)S(1)}, u32[]{:S(2)}, u32[]{:S(2)}) collective-permute-start(f32[1,128]{1,0:T(1,128)S(1)} %add.18), channel_id=1, source_target_pairs={{0,3},{1,2},{2,1},{3,0},{4,7},{5,6},{6,5},{7,4},{8,11},{9,10},{10,... | collective-permute-start | bytes 1544 | tf_op jit(solution)/shard_map/ppermute | solution.py:20
  34.9 0.5 %shard_map.73.carry_ref = f32[128,1152]{1,0:T(8,128)S(1)} custom-call(f32[2,128]{1,0:T(2,128)S(1)} %shard_map.67.par_ref, bf16[128,1152]{1,0:T(8,128)(2,1)S(1)} %shard_map.68.txt_ref.own_ref, f32[128,1152]{1,0:T(8,128)S(1)} %get-tuple-element.18.carry_ref, bf16[128,1152]{1,0:T(8,128)(2,1)S(1)} %collective-permute-done.9.refs_0_), custom_call_target="tpu_custom_call" | custom-call | flops 75497472 | tf_op jit(solution)/shard_map/pallas_call | solution.py:24
  35.4 0.9 %collective-permute-done.7 = f32[1,128]{1,0:T(1,128)S(1)} collective-permute-done((f32[1,128]{1,0:T(1,128)S(1)}, f32[1,128]{1,0:T(1,128)S(1)}, u32[]{:S(2)}, u32[]{:S(2)}) %collective-permute-start.7) | collective-permute-done | bytes 544 | tf_op jit(solution)/shard_map/ppermute | solution.py:20
  36.3 0.5 %add.19 = f32[1,128]{1,0:T(1,128)} add(f32[1,128]{1,0:T(1,128)S(1)} %add.18, f32[1,128]{1,0:T(1,128)S(1)} %collective-permute-done.7) | non-fusion elementwise | flops 128 | bytes 1536 | tf_op jit(solution)/shard_map/add | solution.py:199
  36.9 1.6 %shard_map.72 = f32[128,1152]{1,0:T(8,128)} custom-call(f32[2,128]{1,0:T(2,128)S(1)} %shard_map.67.par_ref, bf16[128,1152]{1,0:T(8,128)(2,1)S(1)} %get-tuple-element.12.img_ref.own_ref, f32[128,1152]{1,0:T(8,128)S(1)} %get-tuple-element.15.carry_ref, f32[128,1152]{1,0:T(8,128)S(1)} %get-tuple-element.16.unit_ref, f32[128,128]{1,0:T(8,128)S(1)} %get-tuple-element.17.inv_ref, ...), custom_call_target="tpu_custom_call" | custom-call | flops 150994944 | tf_op jit(solution)/shard_map/pallas_call | solution.py:24
  38.4 0.0 collective-permute-done.10.refs_0_
  38.4 1.4 %shard_map.75 = f32[128,1152]{1,0:T(8,128)} custom-call(f32[2,128]{1,0:T(2,128)S(1)} %shard_map.67.par_ref, bf16[128,1152]{1,0:T(8,128)(2,1)S(1)} %shard_map.68.txt_ref.own_ref, f32[128,1152]{1,0:T(8,128)S(1)} %shard_map.73.carry_ref, f32[128,1152]{1,0:T(8,128)S(1)} %get-tuple-element.19.unit_ref, f32[128,128]{1,0:T(8,128)S(1)} %get-tuple-element.20.inv_ref, ...), custom_call_target="tpu_custom_call" | custom-call | flops 75497472 | tf_op jit(solution)/shard_map/pallas_call | solution.py:24
  (6 shorter events, 0.0 us)
Async XLA Ops:
  1.9 9.9 %collective-permute-start.2 = (bf16[128,1152]{1,0:T(8,128)(2,1)S(1)}, bf16[128,1152]{1,0:T(8,128)(2,1)S(1)}, u32[]{:S(2)}, u32[]{:S(2)}) collective-permute-start(bf16[128,1152]{1,0:T(8,128)(2,1)S(1)} %shard_map.68.txt_ref.own_ref), channel_id=1, source_target_pairs={{0,3},{1,2},{2,1},{3,0},{4,7},{5,6},{6,5},{7,4},{8,11},{9,10},{10,... | collective-permute-start | bytes 884744 | tf_op jit(solution)/shard_map/ppermute | solution.py:20
  5.6 12.5 %collective-permute-start.9 = (bf16[128,1152]{1,0:T(8,128)(2,1)S(1)}, bf16[128,1152]{1,0:T(8,128)(2,1)S(1)}, u32[]{:S(2)}, u32[]{:S(2)}) collective-permute-start(bf16[128,1152]{1,0:T(8,128)(2,1)S(1)} %get-tuple-element.12.img_ref.own_ref), channel_id=1, source_target_pairs={{0,3},{1,2},{2,1},{3,0},{4,7},{5,6},{6,5},{7,4},{8,11},{9,10},{10,... | collective-permute-start | bytes 884744 | tf_op jit(solution)/shard_map/ppermute | solution.py:20
  5.7 14.0 %collective-permute-start = (bf16[128,1152]{1,0:T(8,128)(2,1)S(1)}, bf16[128,1152]{1,0:T(8,128)(2,1)S(1)}, u32[]{:S(2)}, u32[]{:S(2)}) collective-permute-start(bf16[128,1152]{1,0:T(8,128)(2,1)S(1)} %shard_map.68.txt_ref.own_ref), channel_id=1, source_target_pairs={{0,1},{1,0},{2,3},{3,2},{4,5},{5,4},{6,7},{7,6},{8,9},{9,8},{10,11... | collective-permute-start | bytes 884744 | tf_op jit(solution)/shard_map/ppermute | solution.py:20
  6.4 13.2 %collective-permute-start.1 = (bf16[128,1152]{1,0:T(8,128)(2,1)S(1)}, bf16[128,1152]{1,0:T(8,128)(2,1)S(1)}, u32[]{:S(2)}, u32[]{:S(2)}) collective-permute-start(bf16[128,1152]{1,0:T(8,128)(2,1)S(1)} %get-tuple-element.12.img_ref.own_ref), channel_id=1, source_target_pairs={{0,1},{1,0},{2,3},{3,2},{4,5},{5,4},{6,7},{7,6},{8,9},{9,8},{10,11... | collective-permute-start | bytes 884744 | tf_op jit(solution)/shard_map/ppermute | solution.py:20
  11.7 25.1 %collective-permute-start.8 = (bf16[128,1152]{1,0:T(8,128)(2,1)S(1)}, bf16[128,1152]{1,0:T(8,128)(2,1)S(1)}, u32[]{:S(2)}, u32[]{:S(2)}) collective-permute-start(bf16[128,1152]{1,0:T(8,128)(2,1)S(1)} %collective-permute-done.2.refs_0_), channel_id=1, source_target_pairs={{0,1},{1,0},{2,3},{3,2},{4,5},{5,4},{6,7},{7,6},{8,9},{9,8},{10,11... | collective-permute-start | bytes 884744 | tf_op jit(solution)/shard_map/ppermute | solution.py:20
  18.1 20.4 %collective-permute-start.10 = (bf16[128,1152]{1,0:T(8,128)(2,1)S(1)}, bf16[128,1152]{1,0:T(8,128)(2,1)S(1)}, u32[]{:S(2)}, u32[]{:S(2)}) collective-permute-start(bf16[128,1152]{1,0:T(8,128)(2,1)S(1)} %collective-permute-done.9.refs_0_), channel_id=1, source_target_pairs={{0,1},{1,0},{2,3},{3,2},{4,5},{5,4},{6,7},{7,6},{8,9},{9,8},{10,11... | collective-permute-start | bytes 884744 | tf_op jit(solution)/shard_map/ppermute | solution.py:20
  21.3 1.2 %collective-permute-start.3 = (f32[1,128]{1,0:T(1,128)S(1)}, f32[1,128]{1,0:T(1,128)S(1)}, u32[]{:S(2)}, u32[]{:S(2)}) collective-permute-start(f32[1,128]{1,0:T(1,128)S(1)} %shard_map.71), channel_id=1, source_target_pairs={{0,1},{1,0},{2,3},{3,2},{4,5},{5,4},{6,7},{7,6},{8,9},{9,8},{10,11... | collective-permute-start | bytes 1544 | tf_op jit(solution)/shard_map/ppermute | solution.py:20
  22.6 4.8 %collective-permute-start.4 = (f32[1,128]{1,0:T(1,128)S(1)}, f32[1,128]{1,0:T(1,128)S(1)}, u32[]{:S(2)}, u32[]{:S(2)}) collective-permute-start(f32[1,128]{1,0:T(1,128)S(1)} %add.15), channel_id=1, source_target_pairs={{0,17},{1,16},{2,19},{3,18},{4,21},{5,20},{6,23},{7,22},{8,25},{9,... | collective-permute-start | bytes 1544 | tf_op jit(solution)/shard_map/ppermute | solution.py:20
  27.4 3.0 %collective-permute-start.5 = (f32[1,128]{1,0:T(1,128)S(1)}, f32[1,128]{1,0:T(1,128)S(1)}, u32[]{:S(2)}, u32[]{:S(2)}) collective-permute-start(f32[1,128]{1,0:T(1,128)S(1)} %add.16), channel_id=1, source_target_pairs={{0,9},{1,8},{2,11},{3,10},{4,13},{5,12},{6,15},{7,14},{8,1},{9,0},... | collective-permute-start | bytes 1544 | tf_op jit(solution)/shard_map/ppermute | solution.py:20
  30.4 3.0 %collective-permute-start.6 = (f32[1,128]{1,0:T(1,128)S(1)}, f32[1,128]{1,0:T(1,128)S(1)}, u32[]{:S(2)}, u32[]{:S(2)}) collective-permute-start(f32[1,128]{1,0:T(1,128)S(1)} %add.17), channel_id=1, source_target_pairs={{0,5},{1,4},{2,7},{3,6},{4,1},{5,0},{6,3},{7,2},{8,13},{9,12},{10,... | collective-permute-start | bytes 1544 | tf_op jit(solution)/shard_map/ppermute | solution.py:20
  33.4 3.0 %collective-permute-start.7 = (f32[1,128]{1,0:T(1,128)S(1)}, f32[1,128]{1,0:T(1,128)S(1)}, u32[]{:S(2)}, u32[]{:S(2)}) collective-permute-start(f32[1,128]{1,0:T(1,128)S(1)} %add.18), channel_id=1, source_target_pairs={{0,3},{1,2},{2,1},{3,0},{4,7},{5,6},{6,5},{7,4},{8,11},{9,10},{10,... | collective-permute-start | bytes 1544 | tf_op jit(solution)/shard_map/ppermute | solution.py:20

commit v4 on v3

--- a/solution.py
+++ b/solution.py
@@ -181,7 +181,7 @@
         functools.partial(last_kernel, len(blocks)),
         jax.ShapeDtypeStruct((rows, width), jnp.float32),
         (params, own, carry, unit, inverse, *blocks),
-        [pltpu.VMEM((rows, width), jnp.float32), pltpu.SemaphoreType.DMA((4,))],
+        [pltpu.VMEM((rows, width), jnp.float32), pltpu.SemaphoreType.DMA((2,))],
         out_hbm=True,
         flops=4 * rows * rows * width * len(blocks),
     )
@@ -192,7 +192,8 @@
     if n_row & (n_row - 1) or n_col & (n_col - 1) or n_col < 2:
         return jnp.sum(lax.psum(value, ("row", "col")), axis=1)
     flips = [1]
-    flips += [n_col << k | 1 for k in reversed(range(n_row.bit_length() - 1))]
+    top = n_row.bit_length() - 2
+    flips += [n_col << k | 1 for k in (top, *range(top)) if k >= 0]
     flips += [1 << k | 1 for k in range(1, n_col.bit_length() - 1)]
     for flip in flips:
         other = moved(value, ("row", "col"), lambda i: i ^ flip)

time: 40.1 us -> 40.1 us (level)
  no operation moved by 1% of the time
where the time goes in v4:
time: 40.1 us; the launch traced here: 39.8 us
  waiting for transfers between devices  15.1 us (38%)
  starting transfers between devices  13.1 us (33%)
  Pallas kernels  8.84 us (22%)
  between operations  2.03 us (5%)
  other arithmetic  0.6 us (1%)
    ppermute x11, waiting for transfers between devices, moved(): return lax.ppermute(value, axis, [(i, target(i)) for i in range(count)])  15.1 us
    ppermute x11, starting transfers between devices, moved(): return lax.ppermute(value, axis, [(i, target(i)) for i in range(count)])  13.1 us
    pallas_call x9, Pallas kernels, kernel_call(): pl.pallas_call(body, out_shape=outs, in_specs=[HBM] * in_hbm + [VMEM] * (...  8.84 us
  transfers between devices with their start and end apart: 11, of which 7 were waited for; matrix products, arithmetic and copies ran while one was open for 2% of the time, Pallas kernels for 16%

profile of v4, /device:TPU:0, one launch (start us, length us, event | category | flops | bytes accessed | tf_op | source)
XLA Modules:
  0.0 39.8 jit_solution(11659866672943362458)
XLA Ops:
  0.6 1.2 %shard_map.68.txt_ref.own_ref = bf16[128,1152]{1,0:T(8,128)(2,1)S(1)} custom-call(f32[128,1152]{1,0:T(8,128)} %raw_ref.5), custom_call_target="tpu_custom_call" | custom-call | tf_op jit(solution)/shard_map/pallas_call | solution.py:24
  1.9 2.5 %collective-permute-start.2 = (bf16[128,1152]{1,0:T(8,128)(2,1)S(1)}, bf16[128,1152]{1,0:T(8,128)(2,1)S(1)}, u32[]{:S(2)}, u32[]{:S(2)}) collective-permute-start(bf16[128,1152]{1,0:T(8,128)(2,1)S(1)} %shard_map.68.txt_ref.own_ref), channel_id=1, source_target_pairs={{0,3},{1,2},{2,1},{3,0},{4,7},{5,6},{6,5},{7,4},{8,11},{9,10},{10,... | collective-permute-start | bytes 884744 | tf_op jit(solution)/shard_map/ppermute | solution.py:20
  4.3 1.2 %shard_map.69 = (bf16[128,1152]{1,0:T(8,128)(2,1)S(1)}, f32[128,1152]{1,0:T(8,128)S(1)}, f32[128,128]{1,0:T(8,128)S(1)}) custom-call(f32[128,1152]{1,0:T(8,128)} %raw_ref.4), custom_call_target="tpu_custom_call" | custom-call | tf_op jit(solution)/shard_map/pallas_call | solution.py:24
  5.6 0.1 collective-permute-start.9
  5.7 0.7 %collective-permute-start = (bf16[128,1152]{1,0:T(8,128)(2,1)S(1)}, bf16[128,1152]{1,0:T(8,128)(2,1)S(1)}, u32[]{:S(2)}, u32[]{:S(2)}) collective-permute-start(bf16[128,1152]{1,0:T(8,128)(2,1)S(1)} %shard_map.68.txt_ref.own_ref), channel_id=1, source_target_pairs={{0,1},{1,0},{2,3},{3,2},{4,5},{5,4},{6,7},{7,6},{8,9},{9,8},{10,11... | collective-permute-start | bytes 884744 | tf_op jit(solution)/shard_map/ppermute | solution.py:20
  6.4 0.1 collective-permute-start.1
  6.5 5.3 %collective-permute-done.2.refs_0_ = bf16[128,1152]{1,0:T(8,128)(2,1)S(1)} collective-permute-done((bf16[128,1152]{1,0:T(8,128)(2,1)S(1)}, bf16[128,1152]{1,0:T(8,128)(2,1)S(1)}, u32[]{:S(2)}, u32[]{:S(2)}) %collective-permute-start.2) | collective-permute-done | bytes 294944 | tf_op jit(solution)/shard_map/ppermute | solution.py:20
  11.7 1.1 %collective-permute-start.8 = (bf16[128,1152]{1,0:T(8,128)(2,1)S(1)}, bf16[128,1152]{1,0:T(8,128)(2,1)S(1)}, u32[]{:S(2)}, u32[]{:S(2)}) collective-permute-start(bf16[128,1152]{1,0:T(8,128)(2,1)S(1)} %collective-permute-done.2.refs_0_), channel_id=1, source_target_pairs={{0,1},{1,0},{2,3},{3,2},{4,5},{5,4},{6,7},{7,6},{8,9},{9,8},{10,11... | collective-permute-start | bytes 884744 | tf_op jit(solution)/shard_map/ppermute | solution.py:20
  12.9 5.2 %collective-permute-done.9.refs_0_ = bf16[128,1152]{1,0:T(8,128)(2,1)S(1)} collective-permute-done((bf16[128,1152]{1,0:T(8,128)(2,1)S(1)}, bf16[128,1152]{1,0:T(8,128)(2,1)S(1)}, u32[]{:S(2)}, u32[]{:S(2)}) %collective-permute-start.9) | collective-permute-done | bytes 294944 | tf_op jit(solution)/shard_map/ppermute | solution.py:20
  18.1 0.1 collective-permute-start.10
  19.5 0.1 maximum_bitcast_fusion
  19.6 0.1 broadcast_in_dim.8.from_ref.par_ref
  19.6 0.0 collective-permute-done.refs_0_
  19.6 0.0 collective-permute-done.1.refs_1_
  19.6 1.2 %shard_map.70 = (f32[128,1152]{1,0:T(8,128)S(1)}, f32[128,1152]{1,0:T(8,128)S(1)}, bf16[256,1152]{1,0:T(8,128)(2,1)S(1)}, f32[1,128]{1,0:T(1,128)S(1)}) custom-call(f32[2,128]{1,0:T(2,128)S(1)} %broadcast_in_dim.8.from_ref.par_ref, bf16[128,1152]{1,0:T(8,128)(2,1)S(1)} %shard_map.68.txt_ref.own_ref, bf16[128,1152]{1,0:T(8,128)(2,1)S(1)} %get-tuple-element.12.img_ref.own_ref, ...), custom_call_target="tpu_custom_call" | custom-call | flops 301989888 | tf_op jit(solution)/shard_map/pallas_call | solution.py:24
  20.9 0.5 %shard_map.71 = f32[1,128]{1,0:T(1,128)S(1)} custom-call(f32[2,128]{1,0:T(2,128)S(1)} %shard_map.67.par_ref, f32[1,128]{1,0:T(1,128)S(1)} %get-tuple-element.13.near_ref, bf16[256,1152]{1,0:T(8,128)(2,1)S(1)} %get-tuple-element.14.pair_ref, bf16[128,1152]{1,0:T(8,128)(2,1)S(1)} %collective-permute-done.2.refs_0_), custom_call_target="tpu_custom_call" | custom-call | flops 75497472 | tf_op jit(solution)/shard_map/pallas_call | solution.py:24
  21.3 0.4 %collective-permute-start.3 = (f32[1,128]{1,0:T(1,128)S(1)}, f32[1,128]{1,0:T(1,128)S(1)}, u32[]{:S(2)}, u32[]{:S(2)}) collective-permute-start(f32[1,128]{1,0:T(1,128)S(1)} %shard_map.71), channel_id=1, source_target_pairs={{0,1},{1,0},{2,3},{3,2},{4,5},{5,4},{6,7},{7,6},{8,9},{9,8},{10,11... | collective-permute-start | bytes 1544 | tf_op jit(solution)/shard_map/ppermute | solution.py:20
  21.8 0.8 %collective-permute-done.3 = f32[1,128]{1,0:T(1,128)S(1)} collective-permute-done((f32[1,128]{1,0:T(1,128)S(1)}, f32[1,128]{1,0:T(1,128)S(1)}, u32[]{:S(2)}, u32[]{:S(2)}) %collective-permute-start.3) | collective-permute-done | bytes 544 | tf_op jit(solution)/shard_map/ppermute | solution.py:20
  22.6 3.5 %collective-permute-start.4 = (f32[1,128]{1,0:T(1,128)S(1)}, f32[1,128]{1,0:T(1,128)S(1)}, u32[]{:S(2)}, u32[]{:S(2)}) collective-permute-start(f32[1,128]{1,0:T(1,128)S(1)} %add.15), channel_id=1, source_target_pairs={{0,17},{1,16},{2,19},{3,18},{4,21},{5,20},{6,23},{7,22},{8,25},{9,... | collective-permute-start | bytes 1544 | tf_op jit(solution)/shard_map/ppermute | solution.py:20
  26.1 1.3 %collective-permute-done.4 = f32[1,128]{1,0:T(1,128)S(1)} collective-permute-done((f32[1,128]{1,0:T(1,128)S(1)}, f32[1,128]{1,0:T(1,128)S(1)}, u32[]{:S(2)}, u32[]{:S(2)}) %collective-permute-start.4) | collective-permute-done | bytes 544 | tf_op jit(solution)/shard_map/ppermute | solution.py:20
  27.4 1.5 %collective-permute-start.5 = (f32[1,128]{1,0:T(1,128)S(1)}, f32[1,128]{1,0:T(1,128)S(1)}, u32[]{:S(2)}, u32[]{:S(2)}) collective-permute-start(f32[1,128]{1,0:T(1,128)S(1)} %add.16), channel_id=1, source_target_pairs={{0,5},{1,4},{2,7},{3,6},{4,1},{5,0},{6,3},{7,2},{8,13},{9,12},{10,... | collective-permute-start | bytes 1544 | tf_op jit(solution)/shard_map/ppermute | solution.py:20
  28.9 1.5 %collective-permute-done.5 = f32[1,128]{1,0:T(1,128)S(1)} collective-permute-done((f32[1,128]{1,0:T(1,128)S(1)}, f32[1,128]{1,0:T(1,128)S(1)}, u32[]{:S(2)}, u32[]{:S(2)}) %collective-permute-start.5) | collective-permute-done | bytes 544 | tf_op jit(solution)/shard_map/ppermute | solution.py:20
  30.4 1.6 %collective-permute-start.6 = (f32[1,128]{1,0:T(1,128)S(1)}, f32[1,128]{1,0:T(1,128)S(1)}, u32[]{:S(2)}, u32[]{:S(2)}) collective-permute-start(f32[1,128]{1,0:T(1,128)S(1)} %add.17), channel_id=1, source_target_pairs={{0,9},{1,8},{2,11},{3,10},{4,13},{5,12},{6,15},{7,14},{8,1},{9,0},... | collective-permute-start | bytes 1544 | tf_op jit(solution)/shard_map/ppermute | solution.py:20
  31.9 1.2 %shard_map.74 = (f32[128,1152]{1,0:T(8,128)S(1)}, f32[128,128]{1,0:T(8,128)S(1)}) custom-call(f32[128,1152]{1,0:T(8,128)} %raw_ref.5), custom_call_target="tpu_custom_call" | custom-call | tf_op jit(solution)/shard_map/pallas_call | solution.py:24
  33.2 0.2 collective-permute-done.6
  33.4 1.5 %collective-permute-start.7 = (f32[1,128]{1,0:T(1,128)S(1)}, f32[1,128]{1,0:T(1,128)S(1)}, u32[]{:S(2)}, u32[]{:S(2)}) collective-permute-start(f32[1,128]{1,0:T(1,128)S(1)} %add.18), channel_id=1, source_target_pairs={{0,3},{1,2},{2,1},{3,0},{4,7},{5,6},{6,5},{7,4},{8,11},{9,10},{10,... | collective-permute-start | bytes 1544 | tf_op jit(solution)/shard_map/ppermute | solution.py:20
  34.9 0.5 %shard_map.73.carry_ref = f32[128,1152]{1,0:T(8,128)S(1)} custom-call(f32[2,128]{1,0:T(2,128)S(1)} %shard_map.67.par_ref, bf16[128,1152]{1,0:T(8,128)(2,1)S(1)} %shard_map.68.txt_ref.own_ref, f32[128,1152]{1,0:T(8,128)S(1)} %get-tuple-element.18.carry_ref, bf16[128,1152]{1,0:T(8,128)(2,1)S(1)} %collective-permute-done.9.refs_0_), custom_call_target="tpu_custom_call" | custom-call | flops 75497472 | tf_op jit(solution)/shard_map/pallas_call | solution.py:24
  35.4 0.9 %collective-permute-done.7 = f32[1,128]{1,0:T(1,128)S(1)} collective-permute-done((f32[1,128]{1,0:T(1,128)S(1)}, f32[1,128]{1,0:T(1,128)S(1)}, u32[]{:S(2)}, u32[]{:S(2)}) %collective-permute-start.7) | collective-permute-done | bytes 544 | tf_op jit(solution)/shard_map/ppermute | solution.py:20
  36.3 0.5 %add.19 = f32[1,128]{1,0:T(1,128)} add(f32[1,128]{1,0:T(1,128)S(1)} %add.18, f32[1,128]{1,0:T(1,128)S(1)} %collective-permute-done.7) | non-fusion elementwise | flops 128 | bytes 1536 | tf_op jit(solution)/shard_map/add | solution.py:200
  36.9 0.0 collective-permute-done.8.refs_1_
  36.9 1.5 %shard_map.72 = f32[128,1152]{1,0:T(8,128)} custom-call(f32[2,128]{1,0:T(2,128)S(1)} %shard_map.67.par_ref, bf16[128,1152]{1,0:T(8,128)(2,1)S(1)} %get-tuple-element.12.img_ref.own_ref, f32[128,1152]{1,0:T(8,128)S(1)} %get-tuple-element.15.carry_ref, f32[128,1152]{1,0:T(8,128)S(1)} %get-tuple-element.16.unit_ref, f32[128,128]{1,0:T(8,128)S(1)} %get-tuple-element.17.inv_ref, ...), custom_call_target="tpu_custom_call" | custom-call | flops 150994944 | tf_op jit(solution)/shard_map/pallas_call | solution.py:24
  38.4 1.4 %shard_map.75 = f32[128,1152]{1,0:T(8,128)} custom-call(f32[2,128]{1,0:T(2,128)S(1)} %shard_map.67.par_ref, bf16[128,1152]{1,0:T(8,128)(2,1)S(1)} %shard_map.68.txt_ref.own_ref, f32[128,1152]{1,0:T(8,128)S(1)} %shard_map.73.carry_ref, f32[128,1152]{1,0:T(8,128)S(1)} %get-tuple-element.19.unit_ref, f32[128,128]{1,0:T(8,128)S(1)} %get-tuple-element.20.inv_ref, ...), custom_call_target="tpu_custom_call" | custom-call | flops 75497472 | tf_op jit(solution)/shard_map/pallas_call | solution.py:24
  (6 shorter events, 0.0 us)
Async XLA Ops:
  1.9 9.9 %collective-permute-start.2 = (bf16[128,1152]{1,0:T(8,128)(2,1)S(1)}, bf16[128,1152]{1,0:T(8,128)(2,1)S(1)}, u32[]{:S(2)}, u32[]{:S(2)}) collective-permute-start(bf16[128,1152]{1,0:T(8,128)(2,1)S(1)} %shard_map.68.txt_ref.own_ref), channel_id=1, source_target_pairs={{0,3},{1,2},{2,1},{3,0},{4,7},{5,6},{6,5},{7,4},{8,11},{9,10},{10,... | collective-permute-start | bytes 884744 | tf_op jit(solution)/shard_map/ppermute | solution.py:20
  5.6 12.5 %collective-permute-start.9 = (bf16[128,1152]{1,0:T(8,128)(2,1)S(1)}, bf16[128,1152]{1,0:T(8,128)(2,1)S(1)}, u32[]{:S(2)}, u32[]{:S(2)}) collective-permute-start(bf16[128,1152]{1,0:T(8,128)(2,1)S(1)} %get-tuple-element.12.img_ref.own_ref), channel_id=1, source_target_pairs={{0,3},{1,2},{2,1},{3,0},{4,7},{5,6},{6,5},{7,4},{8,11},{9,10},{10,... | collective-permute-start | bytes 884744 | tf_op jit(solution)/shard_map/ppermute | solution.py:20
  5.7 14.0 %collective-permute-start = (bf16[128,1152]{1,0:T(8,128)(2,1)S(1)}, bf16[128,1152]{1,0:T(8,128)(2,1)S(1)}, u32[]{:S(2)}, u32[]{:S(2)}) collective-permute-start(bf16[128,1152]{1,0:T(8,128)(2,1)S(1)} %shard_map.68.txt_ref.own_ref), channel_id=1, source_target_pairs={{0,1},{1,0},{2,3},{3,2},{4,5},{5,4},{6,7},{7,6},{8,9},{9,8},{10,11... | collective-permute-start | bytes 884744 | tf_op jit(solution)/shard_map/ppermute | solution.py:20
  6.4 13.2 %collective-permute-start.1 = (bf16[128,1152]{1,0:T(8,128)(2,1)S(1)}, bf16[128,1152]{1,0:T(8,128)(2,1)S(1)}, u32[]{:S(2)}, u32[]{:S(2)}) collective-permute-start(bf16[128,1152]{1,0:T(8,128)(2,1)S(1)} %get-tuple-element.12.img_ref.own_ref), channel_id=1, source_target_pairs={{0,1},{1,0},{2,3},{3,2},{4,5},{5,4},{6,7},{7,6},{8,9},{9,8},{10,11... | collective-permute-start | bytes 884744 | tf_op jit(solution)/shard_map/ppermute | solution.py:20
  11.7 25.1 %collective-permute-start.8 = (bf16[128,1152]{1,0:T(8,128)(2,1)S(1)}, bf16[128,1152]{1,0:T(8,128)(2,1)S(1)}, u32[]{:S(2)}, u32[]{:S(2)}) collective-permute-start(bf16[128,1152]{1,0:T(8,128)(2,1)S(1)} %collective-permute-done.2.refs_0_), channel_id=1, source_target_pairs={{0,1},{1,0},{2,3},{3,2},{4,5},{5,4},{6,7},{7,6},{8,9},{9,8},{10,11... | collective-permute-start | bytes 884744 | tf_op jit(solution)/shard_map/ppermute | solution.py:20
  18.1 20.3 %collective-permute-start.10 = (bf16[128,1152]{1,0:T(8,128)(2,1)S(1)}, bf16[128,1152]{1,0:T(8,128)(2,1)S(1)}, u32[]{:S(2)}, u32[]{:S(2)}) collective-permute-start(bf16[128,1152]{1,0:T(8,128)(2,1)S(1)} %collective-permute-done.9.refs_0_), channel_id=1, source_target_pairs={{0,1},{1,0},{2,3},{3,2},{4,5},{5,4},{6,7},{7,6},{8,9},{9,8},{10,11... | collective-permute-start | bytes 884744 | tf_op jit(solution)/shard_map/ppermute | solution.py:20
  21.3 1.2 %collective-permute-start.3 = (f32[1,128]{1,0:T(1,128)S(1)}, f32[1,128]{1,0:T(1,128)S(1)}, u32[]{:S(2)}, u32[]{:S(2)}) collective-permute-start(f32[1,128]{1,0:T(1,128)S(1)} %shard_map.71), channel_id=1, source_target_pairs={{0,1},{1,0},{2,3},{3,2},{4,5},{5,4},{6,7},{7,6},{8,9},{9,8},{10,11... | collective-permute-start | bytes 1544 | tf_op jit(solution)/shard_map/ppermute | solution.py:20
  22.6 4.8 %collective-permute-start.4 = (f32[1,128]{1,0:T(1,128)S(1)}, f32[1,128]{1,0:T(1,128)S(1)}, u32[]{:S(2)}, u32[]{:S(2)}) collective-permute-start(f32[1,128]{1,0:T(1,128)S(1)} %add.15), channel_id=1, source_target_pairs={{0,17},{1,16},{2,19},{3,18},{4,21},{5,20},{6,23},{7,22},{8,25},{9,... | collective-permute-start | bytes 1544 | tf_op jit(solution)/shard_map/ppermute | solution.py:20
  27.4 3.0 %collective-permute-start.5 = (f32[1,128]{1,0:T(1,128)S(1)}, f32[1,128]{1,0:T(1,128)S(1)}, u32[]{:S(2)}, u32[]{:S(2)}) collective-permute-start(f32[1,128]{1,0:T(1,128)S(1)} %add.16), channel_id=1, source_target_pairs={{0,5},{1,4},{2,7},{3,6},{4,1},{5,0},{6,3},{7,2},{8,13},{9,12},{10,... | collective-permute-start | bytes 1544 | tf_op jit(solution)/shard_map/ppermute | solution.py:20
  30.4 3.0 %collective-permute-start.6 = (f32[1,128]{1,0:T(1,128)S(1)}, f32[1,128]{1,0:T(1,128)S(1)}, u32[]{:S(2)}, u32[]{:S(2)}) collective-permute-start(f32[1,128]{1,0:T(1,128)S(1)} %add.17), channel_id=1, source_target_pairs={{0,9},{1,8},{2,11},{3,10},{4,13},{5,12},{6,15},{7,14},{8,1},{9,0},... | collective-permute-start | bytes 1544 | tf_op jit(solution)/shard_map/ppermute | solution.py:20
  33.4 3.0 %collective-permute-start.7 = (f32[1,128]{1,0:T(1,128)S(1)}, f32[1,128]{1,0:T(1,128)S(1)}, u32[]{:S(2)}, u32[]{:S(2)}) collective-permute-start(f32[1,128]{1,0:T(1,128)S(1)} %add.18), channel_id=1, source_target_pairs={{0,3},{1,2},{2,1},{3,0},{4,7},{5,6},{6,5},{7,4},{8,11},{9,10},{10,... | collective-permute-start | bytes 1544 | tf_op jit(solution)/shard_map/ppermute | solution.py:20

commit v5 on v4

--- a/solution.py
+++ b/solution.py
@@ -191,10 +191,9 @@
     n_row, n_col = lax.axis_size("row"), lax.axis_size("col")
     if n_row & (n_row - 1) or n_col & (n_col - 1) or n_col < 2:
         return jnp.sum(lax.psum(value, ("row", "col")), axis=1)
-    flips = [1]
     top = n_row.bit_length() - 2
-    flips += [n_col << k | 1 for k in (top, *range(top)) if k >= 0]
-    flips += [1 << k | 1 for k in range(1, n_col.bit_length() - 1)]
+    rows = [n_col << k | 1 for k in (top, *reversed(range(top))) if k >= 0]
+    flips = [1, *rows[:1], *(1 << k | 1 for k in range(1, n_col.bit_length() - 1)), *rows[1:]]
     for flip in flips:
         other = moved(value, ("row", "col"), lambda i: i ^ flip)
         value = value + other

time: 40.1 us -> 40.1 us (level)
  no operation moved by 1% of the time
where the time goes in v5:
time: 40.1 us; the launch traced here: 39.8 us
  waiting for transfers between devices  15.1 us (38%)
  starting transfers between devices  13.1 us (33%)
  Pallas kernels  8.84 us (22%)
  between operations  2.03 us (5%)
  other arithmetic  0.6 us (1%)
    ppermute x11, waiting for transfers between devices, moved(): return lax.ppermute(value, axis, [(i, target(i)) for i in range(count)])  15.1 us
    ppermute x11, starting transfers between devices, moved(): return lax.ppermute(value, axis, [(i, target(i)) for i in range(count)])  13.1 us
    pallas_call x9, Pallas kernels, kernel_call(): pl.pallas_call(body, out_shape=outs, in_specs=[HBM] * in_hbm + [VMEM] * (...  8.84 us
  transfers between devices with their start and end apart: 11, of which 7 were waited for; matrix products, arithmetic and copies ran while one was open for 2% of the time, Pallas kernels for 16%

profile of v5, /device:TPU:0, one launch (start us, length us, event | category | flops | bytes accessed | tf_op | source)
XLA Modules:
  0.0 39.8 jit_solution(4580449563947315087)
XLA Ops:
  0.6 1.2 %shard_map.68.txt_ref.own_ref = bf16[128,1152]{1,0:T(8,128)(2,1)S(1)} custom-call(f32[128,1152]{1,0:T(8,128)} %raw_ref.5), custom_call_target="tpu_custom_call" | custom-call | tf_op jit(solution)/shard_map/pallas_call | solution.py:24
  1.9 2.5 %collective-permute-start.2 = (bf16[128,1152]{1,0:T(8,128)(2,1)S(1)}, bf16[128,1152]{1,0:T(8,128)(2,1)S(1)}, u32[]{:S(2)}, u32[]{:S(2)}) collective-permute-start(bf16[128,1152]{1,0:T(8,128)(2,1)S(1)} %shard_map.68.txt_ref.own_ref), channel_id=1, source_target_pairs={{0,3},{1,2},{2,1},{3,0},{4,7},{5,6},{6,5},{7,4},{8,11},{9,10},{10,... | collective-permute-start | bytes 884744 | tf_op jit(solution)/shard_map/ppermute | solution.py:20
  4.3 1.2 %shard_map.69 = (bf16[128,1152]{1,0:T(8,128)(2,1)S(1)}, f32[128,1152]{1,0:T(8,128)S(1)}, f32[128,128]{1,0:T(8,128)S(1)}) custom-call(f32[128,1152]{1,0:T(8,128)} %raw_ref.4), custom_call_target="tpu_custom_call" | custom-call | tf_op jit(solution)/shard_map/pallas_call | solution.py:24
  5.6 0.1 collective-permute-start.9
  5.7 0.7 %collective-permute-start = (bf16[128,1152]{1,0:T(8,128)(2,1)S(1)}, bf16[128,1152]{1,0:T(8,128)(2,1)S(1)}, u32[]{:S(2)}, u32[]{:S(2)}) collective-permute-start(bf16[128,1152]{1,0:T(8,128)(2,1)S(1)} %shard_map.68.txt_ref.own_ref), channel_id=1, source_target_pairs={{0,1},{1,0},{2,3},{3,2},{4,5},{5,4},{6,7},{7,6},{8,9},{9,8},{10,11... | collective-permute-start | bytes 884744 | tf_op jit(solution)/shard_map/ppermute | solution.py:20
  6.4 0.1 collective-permute-start.1
  6.5 5.3 %collective-permute-done.2.refs_0_ = bf16[128,1152]{1,0:T(8,128)(2,1)S(1)} collective-permute-done((bf16[128,1152]{1,0:T(8,128)(2,1)S(1)}, bf16[128,1152]{1,0:T(8,128)(2,1)S(1)}, u32[]{:S(2)}, u32[]{:S(2)}) %collective-permute-start.2) | collective-permute-done | bytes 294944 | tf_op jit(solution)/shard_map/ppermute | solution.py:20
  11.7 1.1 %collective-permute-start.8 = (bf16[128,1152]{1,0:T(8,128)(2,1)S(1)}, bf16[128,1152]{1,0:T(8,128)(2,1)S(1)}, u32[]{:S(2)}, u32[]{:S(2)}) collective-permute-start(bf16[128,1152]{1,0:T(8,128)(2,1)S(1)} %collective-permute-done.2.refs_0_), channel_id=1, source_target_pairs={{0,1},{1,0},{2,3},{3,2},{4,5},{5,4},{6,7},{7,6},{8,9},{9,8},{10,11... | collective-permute-start | bytes 884744 | tf_op jit(solution)/shard_map/ppermute | solution.py:20
  12.9 5.2 %collective-permute-done.9.refs_0_ = bf16[128,1152]{1,0:T(8,128)(2,1)S(1)} collective-permute-done((bf16[128,1152]{1,0:T(8,128)(2,1)S(1)}, bf16[128,1152]{1,0:T(8,128)(2,1)S(1)}, u32[]{:S(2)}, u32[]{:S(2)}) %collective-permute-start.9) | collective-permute-done | bytes 294944 | tf_op jit(solution)/shard_map/ppermute | solution.py:20
  18.1 0.1 collective-permute-start.10
  19.5 0.1 maximum_bitcast_fusion
  19.6 0.1 broadcast_in_dim.8.from_ref.par_ref
  19.6 0.0 collective-permute-done.refs_0_
  19.6 0.0 collective-permute-done.1.refs_1_
  19.6 1.2 %shard_map.70 = (f32[128,1152]{1,0:T(8,128)S(1)}, f32[128,1152]{1,0:T(8,128)S(1)}, bf16[256,1152]{1,0:T(8,128)(2,1)S(1)}, f32[1,128]{1,0:T(1,128)S(1)}) custom-call(f32[2,128]{1,0:T(2,128)S(1)} %broadcast_in_dim.8.from_ref.par_ref, bf16[128,1152]{1,0:T(8,128)(2,1)S(1)} %shard_map.68.txt_ref.own_ref, bf16[128,1152]{1,0:T(8,128)(2,1)S(1)} %get-tuple-element.12.img_ref.own_ref, ...), custom_call_target="tpu_custom_call" | custom-call | flops 301989888 | tf_op jit(solution)/shard_map/pallas_call | solution.py:24
  20.9 0.5 %shard_map.71 = f32[1,128]{1,0:T(1,128)S(1)} custom-call(f32[2,128]{1,0:T(2,128)S(1)} %shard_map.67.par_ref, f32[1,128]{1,0:T(1,128)S(1)} %get-tuple-element.13.near_ref, bf16[256,1152]{1,0:T(8,128)(2,1)S(1)} %get-tuple-element.14.pair_ref, bf16[128,1152]{1,0:T(8,128)(2,1)S(1)} %collective-permute-done.2.refs_0_), custom_call_target="tpu_custom_call" | custom-call | flops 75497472 | tf_op jit(solution)/shard_map/pallas_call | solution.py:24
  21.3 0.4 %collective-permute-start.3 = (f32[1,128]{1,0:T(1,128)S(1)}, f32[1,128]{1,0:T(1,128)S(1)}, u32[]{:S(2)}, u32[]{:S(2)}) collective-permute-start(f32[1,128]{1,0:T(1,128)S(1)} %shard_map.71), channel_id=1, source_target_pairs={{0,1},{1,0},{2,3},{3,2},{4,5},{5,4},{6,7},{7,6},{8,9},{9,8},{10,11... | collective-permute-start | bytes 1544 | tf_op jit(solution)/shard_map/ppermute | solution.py:20
  21.8 0.8 %collective-permute-done.3 = f32[1,128]{1,0:T(1,128)S(1)} collective-permute-done((f32[1,128]{1,0:T(1,128)S(1)}, f32[1,128]{1,0:T(1,128)S(1)}, u32[]{:S(2)}, u32[]{:S(2)}) %collective-permute-start.3) | collective-permute-done | bytes 544 | tf_op jit(solution)/shard_map/ppermute | solution.py:20
  22.6 3.5 %collective-permute-start.4 = (f32[1,128]{1,0:T(1,128)S(1)}, f32[1,128]{1,0:T(1,128)S(1)}, u32[]{:S(2)}, u32[]{:S(2)}) collective-permute-start(f32[1,128]{1,0:T(1,128)S(1)} %add.15), channel_id=1, source_target_pairs={{0,17},{1,16},{2,19},{3,18},{4,21},{5,20},{6,23},{7,22},{8,25},{9,... | collective-permute-start | bytes 1544 | tf_op jit(solution)/shard_map/ppermute | solution.py:20
  26.1 1.3 %collective-permute-done.4 = f32[1,128]{1,0:T(1,128)S(1)} collective-permute-done((f32[1,128]{1,0:T(1,128)S(1)}, f32[1,128]{1,0:T(1,128)S(1)}, u32[]{:S(2)}, u32[]{:S(2)}) %collective-permute-start.4) | collective-permute-done | bytes 544 | tf_op jit(solution)/shard_map/ppermute | solution.py:20
  27.4 1.5 %collective-permute-start.5 = (f32[1,128]{1,0:T(1,128)S(1)}, f32[1,128]{1,0:T(1,128)S(1)}, u32[]{:S(2)}, u32[]{:S(2)}) collective-permute-start(f32[1,128]{1,0:T(1,128)S(1)} %add.16), channel_id=1, source_target_pairs={{0,3},{1,2},{2,1},{3,0},{4,7},{5,6},{6,5},{7,4},{8,11},{9,10},{10,... | collective-permute-start | bytes 1544 | tf_op jit(solution)/shard_map/ppermute | solution.py:20
  28.9 1.5 %collective-permute-done.5 = f32[1,128]{1,0:T(1,128)S(1)} collective-permute-done((f32[1,128]{1,0:T(1,128)S(1)}, f32[1,128]{1,0:T(1,128)S(1)}, u32[]{:S(2)}, u32[]{:S(2)}) %collective-permute-start.5) | collective-permute-done | bytes 544 | tf_op jit(solution)/shard_map/ppermute | solution.py:20
  30.4 1.6 %collective-permute-start.6 = (f32[1,128]{1,0:T(1,128)S(1)}, f32[1,128]{1,0:T(1,128)S(1)}, u32[]{:S(2)}, u32[]{:S(2)}) collective-permute-start(f32[1,128]{1,0:T(1,128)S(1)} %add.17), channel_id=1, source_target_pairs={{0,9},{1,8},{2,11},{3,10},{4,13},{5,12},{6,15},{7,14},{8,1},{9,0},... | collective-permute-start | bytes 1544 | tf_op jit(solution)/shard_map/ppermute | solution.py:20
  31.9 1.2 %shard_map.74 = (f32[128,1152]{1,0:T(8,128)S(1)}, f32[128,128]{1,0:T(8,128)S(1)}) custom-call(f32[128,1152]{1,0:T(8,128)} %raw_ref.5), custom_call_target="tpu_custom_call" | custom-call | tf_op jit(solution)/shard_map/pallas_call | solution.py:24
  33.2 0.2 collective-permute-done.6
  33.4 1.5 %collective-permute-start.7 = (f32[1,128]{1,0:T(1,128)S(1)}, f32[1,128]{1,0:T(1,128)S(1)}, u32[]{:S(2)}, u32[]{:S(2)}) collective-permute-start(f32[1,128]{1,0:T(1,128)S(1)} %add.18), channel_id=1, source_target_pairs={{0,5},{1,4},{2,7},{3,6},{4,1},{5,0},{6,3},{7,2},{8,13},{9,12},{10,... | collective-permute-start | bytes 1544 | tf_op jit(solution)/shard_map/ppermute | solution.py:20
  34.9 0.5 %shard_map.73.carry_ref = f32[128,1152]{1,0:T(8,128)S(1)} custom-call(f32[2,128]{1,0:T(2,128)S(1)} %shard_map.67.par_ref, bf16[128,1152]{1,0:T(8,128)(2,1)S(1)} %shard_map.68.txt_ref.own_ref, f32[128,1152]{1,0:T(8,128)S(1)} %get-tuple-element.18.carry_ref, bf16[128,1152]{1,0:T(8,128)(2,1)S(1)} %collective-permute-done.9.refs_0_), custom_call_target="tpu_custom_call" | custom-call | flops 75497472 | tf_op jit(solution)/shard_map/pallas_call | solution.py:24
  35.4 0.9 %collective-permute-done.7 = f32[1,128]{1,0:T(1,128)S(1)} collective-permute-done((f32[1,128]{1,0:T(1,128)S(1)}, f32[1,128]{1,0:T(1,128)S(1)}, u32[]{:S(2)}, u32[]{:S(2)}) %collective-permute-start.7) | collective-permute-done | bytes 544 | tf_op jit(solution)/shard_map/ppermute | solution.py:20
  36.3 0.5 %add.19 = f32[1,128]{1,0:T(1,128)} add(f32[1,128]{1,0:T(1,128)S(1)} %add.18, f32[1,128]{1,0:T(1,128)S(1)} %collective-permute-done.7) | non-fusion elementwise | flops 128 | bytes 1536 | tf_op jit(solution)/shard_map/add | solution.py:199
  36.9 0.0 collective-permute-done.8.refs_1_
  36.9 1.5 %shard_map.72 = f32[128,1152]{1,0:T(8,128)} custom-call(f32[2,128]{1,0:T(2,128)S(1)} %shard_map.67.par_ref, bf16[128,1152]{1,0:T(8,128)(2,1)S(1)} %get-tuple-element.12.img_ref.own_ref, f32[128,1152]{1,0:T(8,128)S(1)} %get-tuple-element.15.carry_ref, f32[128,1152]{1,0:T(8,128)S(1)} %get-tuple-element.16.unit_ref, f32[128,128]{1,0:T(8,128)S(1)} %get-tuple-element.17.inv_ref, ...), custom_call_target="tpu_custom_call" | custom-call | flops 150994944 | tf_op jit(solution)/shard_map/pallas_call | solution.py:24
  38.4 1.4 %shard_map.75 = f32[128,1152]{1,0:T(8,128)} custom-call(f32[2,128]{1,0:T(2,128)S(1)} %shard_map.67.par_ref, bf16[128,1152]{1,0:T(8,128)(2,1)S(1)} %shard_map.68.txt_ref.own_ref, f32[128,1152]{1,0:T(8,128)S(1)} %shard_map.73.carry_ref, f32[128,1152]{1,0:T(8,128)S(1)} %get-tuple-element.19.unit_ref, f32[128,128]{1,0:T(8,128)S(1)} %get-tuple-element.20.inv_ref, ...), custom_call_target="tpu_custom_call" | custom-call | flops 75497472 | tf_op jit(solution)/shard_map/pallas_call | solution.py:24
  (6 shorter events, 0.0 us)
Async XLA Ops:
  1.9 9.9 %collective-permute-start.2 = (bf16[128,1152]{1,0:T(8,128)(2,1)S(1)}, bf16[128,1152]{1,0:T(8,128)(2,1)S(1)}, u32[]{:S(2)}, u32[]{:S(2)}) collective-permute-start(bf16[128,1152]{1,0:T(8,128)(2,1)S(1)} %shard_map.68.txt_ref.own_ref), channel_id=1, source_target_pairs={{0,3},{1,2},{2,1},{3,0},{4,7},{5,6},{6,5},{7,4},{8,11},{9,10},{10,... | collective-permute-start | bytes 884744 | tf_op jit(solution)/shard_map/ppermute | solution.py:20
  5.6 12.5 %collective-permute-start.9 = (bf16[128,1152]{1,0:T(8,128)(2,1)S(1)}, bf16[128,1152]{1,0:T(8,128)(2,1)S(1)}, u32[]{:S(2)}, u32[]{:S(2)}) collective-permute-start(bf16[128,1152]{1,0:T(8,128)(2,1)S(1)} %get-tuple-element.12.img_ref.own_ref), channel_id=1, source_target_pairs={{0,3},{1,2},{2,1},{3,0},{4,7},{5,6},{6,5},{7,4},{8,11},{9,10},{10,... | collective-permute-start | bytes 884744 | tf_op jit(solution)/shard_map/ppermute | solution.py:20
  5.7 14.0 %collective-permute-start = (bf16[128,1152]{1,0:T(8,128)(2,1)S(1)}, bf16[128,1152]{1,0:T(8,128)(2,1)S(1)}, u32[]{:S(2)}, u32[]{:S(2)}) collective-permute-start(bf16[128,1152]{1,0:T(8,128)(2,1)S(1)} %shard_map.68.txt_ref.own_ref), channel_id=1, source_target_pairs={{0,1},{1,0},{2,3},{3,2},{4,5},{5,4},{6,7},{7,6},{8,9},{9,8},{10,11... | collective-permute-start | bytes 884744 | tf_op jit(solution)/shard_map/ppermute | solution.py:20
  6.4 13.2 %collective-permute-start.1 = (bf16[128,1152]{1,0:T(8,128)(2,1)S(1)}, bf16[128,1152]{1,0:T(8,128)(2,1)S(1)}, u32[]{:S(2)}, u32[]{:S(2)}) collective-permute-start(bf16[128,1152]{1,0:T(8,128)(2,1)S(1)} %get-tuple-element.12.img_ref.own_ref), channel_id=1, source_target_pairs={{0,1},{1,0},{2,3},{3,2},{4,5},{5,4},{6,7},{7,6},{8,9},{9,8},{10,11... | collective-permute-start | bytes 884744 | tf_op jit(solution)/shard_map/ppermute | solution.py:20
  11.7 25.1 %collective-permute-start.8 = (bf16[128,1152]{1,0:T(8,128)(2,1)S(1)}, bf16[128,1152]{1,0:T(8,128)(2,1)S(1)}, u32[]{:S(2)}, u32[]{:S(2)}) collective-permute-start(bf16[128,1152]{1,0:T(8,128)(2,1)S(1)} %collective-permute-done.2.refs_0_), channel_id=1, source_target_pairs={{0,1},{1,0},{2,3},{3,2},{4,5},{5,4},{6,7},{7,6},{8,9},{9,8},{10,11... | collective-permute-start | bytes 884744 | tf_op jit(solution)/shard_map/ppermute | solution.py:20
  18.1 20.3 %collective-permute-start.10 = (bf16[128,1152]{1,0:T(8,128)(2,1)S(1)}, bf16[128,1152]{1,0:T(8,128)(2,1)S(1)}, u32[]{:S(2)}, u32[]{:S(2)}) collective-permute-start(bf16[128,1152]{1,0:T(8,128)(2,1)S(1)} %collective-permute-done.9.refs_0_), channel_id=1, source_target_pairs={{0,1},{1,0},{2,3},{3,2},{4,5},{5,4},{6,7},{7,6},{8,9},{9,8},{10,11... | collective-permute-start | bytes 884744 | tf_op jit(solution)/shard_map/ppermute | solution.py:20
  21.3 1.2 %collective-permute-start.3 = (f32[1,128]{1,0:T(1,128)S(1)}, f32[1,128]{1,0:T(1,128)S(1)}, u32[]{:S(2)}, u32[]{:S(2)}) collective-permute-start(f32[1,128]{1,0:T(1,128)S(1)} %shard_map.71), channel_id=1, source_target_pairs={{0,1},{1,0},{2,3},{3,2},{4,5},{5,4},{6,7},{7,6},{8,9},{9,8},{10,11... | collective-permute-start | bytes 1544 | tf_op jit(solution)/shard_map/ppermute | solution.py:20
  22.6 4.8 %collective-permute-start.4 = (f32[1,128]{1,0:T(1,128)S(1)}, f32[1,128]{1,0:T(1,128)S(1)}, u32[]{:S(2)}, u32[]{:S(2)}) collective-permute-start(f32[1,128]{1,0:T(1,128)S(1)} %add.15), channel_id=1, source_target_pairs={{0,17},{1,16},{2,19},{3,18},{4,21},{5,20},{6,23},{7,22},{8,25},{9,... | collective-permute-start | bytes 1544 | tf_op jit(solution)/shard_map/ppermute | solution.py:20
  27.4 3.0 %collective-permute-start.5 = (f32[1,128]{1,0:T(1,128)S(1)}, f32[1,128]{1,0:T(1,128)S(1)}, u32[]{:S(2)}, u32[]{:S(2)}) collective-permute-start(f32[1,128]{1,0:T(1,128)S(1)} %add.16), channel_id=1, source_target_pairs={{0,3},{1,2},{2,1},{3,0},{4,7},{5,6},{6,5},{7,4},{8,11},{9,10},{10,... | collective-permute-start | bytes 1544 | tf_op jit(solution)/shard_map/ppermute | solution.py:20
  30.4 3.0 %collective-permute-start.6 = (f32[1,128]{1,0:T(1,128)S(1)}, f32[1,128]{1,0:T(1,128)S(1)}, u32[]{:S(2)}, u32[]{:S(2)}) collective-permute-start(f32[1,128]{1,0:T(1,128)S(1)} %add.17), channel_id=1, source_target_pairs={{0,9},{1,8},{2,11},{3,10},{4,13},{5,12},{6,15},{7,14},{8,1},{9,0},... | collective-permute-start | bytes 1544 | tf_op jit(solution)/shard_map/ppermute | solution.py:20
  33.4 3.0 %collective-permute-start.7 = (f32[1,128]{1,0:T(1,128)S(1)}, f32[1,128]{1,0:T(1,128)S(1)}, u32[]{:S(2)}, u32[]{:S(2)}) collective-permute-start(f32[1,128]{1,0:T(1,128)S(1)} %add.18), channel_id=1, source_target_pairs={{0,5},{1,4},{2,7},{3,6},{4,1},{5,0},{6,3},{7,2},{8,13},{9,12},{10,... | collective-permute-start | bytes 1544 | tf_op jit(solution)/shard_map/ppermute | solution.py:20
